TPU v7x, 32 devices: a whole 2x2x4 slice. The times are simulated.
32 devices in a mesh: groups: 2 (over y), dp: 4 (over z), tensor: 4 (over x, core).
Axes of the slice: x: 2, y: 2, z: 4, core: 2. Of those that a mesh axis runs over, the one named last changes fastest.
Arguments:
- tokens: bfloat16 [4096, 4096], P(('groups', 'dp')), parts along dimension 0, may hold values from -6 to 6
- w_query: bfloat16 [4096, 4096], P('dp', 'tensor'), may hold values from -0.09375 to 0.09375
- w_key: bfloat16 [4096, 1024], P('dp', 'tensor'), may hold values from -0.09375 to 0.09375
- w_value: bfloat16 [4096, 1024], P('dp', 'tensor'), may hold values from -0.09375 to 0.09375
- a_query: bfloat16 [8, 4096, 32], P(('groups', 'dp'), 'tensor'), parts along dimension 0, may hold values from -0.09375 to 0.09375
- b_query: bfloat16 [8, 32, 4096], P(('groups', 'dp'), None, 'tensor'), parts along dimension 0, may hold values from -1 to 1
- a_value: bfloat16 [8, 4096, 32], P(('groups', 'dp'), 'tensor'), parts along dimension 0, may hold values from -0.09375 to 0.09375
- b_value: bfloat16 [8, 32, 1024], P(('groups', 'dp'), None, 'tensor'), parts along dimension 0, may hold values from -1 to 1
- adapter_ranks: int32 [8], P('groups'), parts along dimension 0, may hold values from 16 to 32
- adapter_slot: int32 [4], replicated, may hold values from 0 to 3, each once
- block_adapter: int32 [32, 1], P(('groups', 'dp')), parts along dimension 0, may hold values from 0 to 3
- live_tokens: int32 [8], P(('groups', 'dp')), parts along dimension 0, may hold values from 1 to 512, 1280 in all
- d_heads: bfloat16 [4096, 4096], P(('groups', 'dp'), 'tensor'), parts along dimension 0, may hold values from -0.29882812 to 0.29882812
Outputs:
- grad_a_query: float32 [8, 4096, 32], P(('groups', 'dp'), 'tensor'), parts along dimension 0
- grad_b_query: float32 [8, 32, 4096], P(('groups', 'dp'), None, 'tensor'), parts along dimension 0
- grad_a_value: float32 [8, 4096, 32], P(('groups', 'dp'), 'tensor'), parts along dimension 0
- grad_b_value: float32 [8, 32, 1024], P(('groups', 'dp'), None, 'tensor'), parts along dimension 0
There are 2 independent parts, one for each index of `groups`. A program takes and returns all parts, laid end to end along the dimension named above; an argument that names none is the same for every part. Nothing has to cross between parts.
Inputs may be any that keep to these rules, and one draw needn't show every extreme that they name: `adapter_slot`: each slot holds exactly one adapter. `block_adapter`: every adapter is named by some block. `live_tokens`: one index of dp has all its rows live.
All inputs are finite; a program needn't handle non-finite values. No bound on the sum of `live_tokens` on one device may be relied on, other than what follows from the above.
Results may differ from a plain program's by a relative error of at most 0.02.
Values may be sent and summed in bfloat16 or wider, within the bound.
A program may use at most 64 MiB of HBM per device.

v0:
```python
import functools

import jax
import jax.numpy as jnp
import numpy as np
from jax import lax
from jax.experimental import pallas as pl
from jax.experimental.pallas import tpu as pltpu
from jax.sharding import PartitionSpec as P

HD = 128
R = 32
REQUEST_ROWS = 128
MESH = pl.DeviceIdType.MESH


adapter_alpha_factor = 32.0
rope_theta = 500000.0


def rope_tables(length, width):
    halfway = width // 2
    spread = rope_theta ** (-2.0 * np.arange(halfway, dtype=np.float32) / width)
    angle = np.arange(length, dtype=np.float32)[:, None] * spread.astype(np.float32)[None, :]
    return np.cos(angle).astype(np.float32), np.sin(angle).astype(np.float32)


def scale_of(rank):
    return (adapter_alpha_factor / jnp.full((1, 128), rank, jnp.int32).astype(jnp.float32))[:, :1]


def greet(axes):
    barrier = pltpu.get_barrier_semaphore()
    total = 0
    for axis in axes:
        size = lax.axis_size(axis)
        me = lax.axis_index(axis)

        @pl.loop(1, size)
        def _(j):
            pl.semaphore_signal(
                barrier, inc=1, device_id={axis: lax.rem(me + j, size)}, device_id_type=MESH
            )

        total += size - 1
    pl.semaphore_wait(barrier, total)


def project_kernel(
    pieces,
    block_ref,
    slot_ref,
    rank_ref,
    x_hbm,
    wq_hbm,
    wk_hbm,
    wv_hbm,
    down_ref,
    bq_ref,
    bv_ref,
    acc_ref,
    u_ref,
    bq_sel_ref,
    bv_sel_ref,
    x_ref,
    w_all,
    down_all,
    bq_all,
    bv_all,
    parts,
    local_sem,
    z_send,
    z_recv,
    y_send,
    y_recv,
    f_send,
    f_recv,
    u_send,
    u_recv,
):
    n = lax.axis_size("dp")
    ng = lax.axis_size("groups")
    nt = lax.axis_size("tensor")
    me = lax.axis_index("dp")
    g = lax.axis_index("groups")
    t = lax.axis_index("tensor")
    depth = w_all.shape[1]
    cols = w_all.shape[2]
    qcols = wq_hbm.shape[1]
    kcols = wk_hbm.shape[1]
    half = depth // ng
    step = half // pieces
    rows = x_ref.shape[0]
    width = down_ref.shape[1]
    block_count = rows // REQUEST_ROWS

    x_copy = pltpu.make_async_copy(x_hbm, x_ref, local_sem.at[0])
    w_copies = [
        pltpu.make_async_copy(src, w_all.at[me, :, pl.ds(at, src.shape[1])], local_sem.at[1 + i])
        for i, (src, at) in enumerate(((wq_hbm, 0), (wk_hbm, qcols), (wv_hbm, qcols + kcols)))
    ]
    f_copies = [
        pltpu.make_async_copy(src, dst.at[me], local_sem.at[4 + i])
        for i, (src, dst) in enumerate(((down_ref, down_all), (bq_ref, bq_all), (bv_ref, bv_all)))
    ]
    for copy in w_copies + f_copies + [x_copy]:
        copy.start()
    greet(("dp", "tensor", "groups"))

    def factor_copies(j, arriving):
        peer = lax.rem(me + n - j, n) if arriving else lax.rem(me + j, n)
        at = peer if arriving else me
        return [
            pltpu.make_async_remote_copy(
                src_ref=src,
                dst_ref=dst.at[at],
                send_sem=f_send.at[i, j],
                recv_sem=f_recv.at[i, j],
                device_id={"dp": peer},
                device_id_type=MESH,
            )
            for i, (src, dst) in enumerate(
                ((down_ref, down_all), (bq_ref, bq_all), (bv_ref, bv_all))
            )
        ]

    @pl.loop(1, n)
    def _(j):
        for copy in factor_copies(j, False):
            copy.start()

    def piece(s, owner, p):
        return w_all.at[s, pl.ds(pl.multiple_of(owner * half + p * step, step), step), :]

    def z_copy(s, p, way):
        target = jnp.clip(me + (1 if way == 0 else -1), 0, n - 1)
        return pltpu.make_async_remote_copy(
            src_ref=piece(s, g, p),
            dst_ref=piece(s, g, p),
            send_sem=z_send.at[way, s, p],
            recv_sem=z_recv.at[s, p],
            device_id={"dp": target},
            device_id_type=MESH,
        )

    def y_copy(s, p, j, arriving):
        owner = lax.rem(g + ng - j, ng) if arriving else g
        return pltpu.make_async_remote_copy(
            src_ref=piece(s, owner, p),
            dst_ref=piece(s, owner, p),
            send_sem=y_send.at[j, s, p],
            recv_sem=y_recv.at[j, s, p],
            device_id={"groups": lax.rem(g + j, ng)},
            device_id_type=MESH,
        )

    for copy in w_copies:
        copy.wait()

    @pl.when(me < n - 1)
    def _():
        for p in range(pieces):
            z_copy(me, p, 0).start()

    @pl.when(me > 0)
    def _():
        for p in range(pieces):
            z_copy(me, p, 1).start()

    tile = 256 if cols % 256 == 0 else 128

    def multiply(s):
        ks = pl.ds(pl.multiple_of(s * depth, 128), depth)

        @pl.loop(0, cols // tile)
        def _(c):
            cs = pl.ds(pl.multiple_of(c * tile, tile), tile)
            acc_ref[:, cs] += jnp.dot(
                x_ref[:, ks], w_all[s, :, cs], preferred_element_type=jnp.float32
            )

    x_copy.wait()
    for copy in f_copies:
        copy.wait()
    acc_ref[...] = jnp.zeros_like(acc_ref)

    @pl.loop(1, n)
    def _(j):
        for copy in factor_copies(j, True):
            copy.wait_recv()

    mine = pl.ds(pl.multiple_of(t * width, 128), width)
    for b in range(block_count):
        span = pl.ds(b * REQUEST_ROWS, REQUEST_ROWS)
        slot = slot_ref[block_ref[b, 0]]
        parts[t, span, :] = lax.dot_general(
            x_ref[span, mine],
            down_all[slot],
            (((1,), (1,)), ((), ())),
            preferred_element_type=jnp.float32,
        )
        bq_sel_ref[b] = bq_all[slot]
        bv_sel_ref[b] = bv_all[slot]

    multiply(me)

    def part_copy(j, arriving):
        peer = lax.rem(t + nt - j, nt) if arriving else lax.rem(t + j, nt)
        at = peer if arriving else t
        return pltpu.make_async_remote_copy(
            src_ref=parts.at[at],
            dst_ref=parts.at[at],
            send_sem=u_send.at[j],
            recv_sem=u_recv.at[j],
            device_id={"tensor": peer},
            device_id_type=MESH,
        )

    for j in range(1, nt):
        part_copy(j, False).start()

    def finish(s, valid):
        @pl.when(valid)
        def _():
            for p in range(pieces):
                for j in range(1, ng):
                    y_copy(s, p, j, True).wait_recv()
            multiply(s)

    def both(d):
        for p in range(pieces):
            for way in (0, 1):
                s = me - d if way == 0 else me + d
                valid = (s >= 0) if way == 0 else (s < n)
                onward = (me < n - 1) if way == 0 else (me > 0)

                @pl.when(valid)
                def _():
                    z_copy(s, p, way).wait_recv()

                    @pl.when(onward)
                    def _():
                        z_copy(s, p, way).start()

                    for j in range(1, ng):
                        y_copy(s, p, j, False).start()

    both(1)

    for j in range(1, nt):
        part_copy(j, True).wait_recv()
    for b in range(block_count):
        span = pl.ds(b * REQUEST_ROWS, REQUEST_ROWS)
        rank = rank_ref[block_ref[b, 0]]
        scale = scale_of(rank)
        total = parts[0, span, :]
        for j in range(1, nt):
            total = total + parts[j, span, :]
        lane = lax.broadcasted_iota(jnp.int32, total.shape, 1)
        lane = jnp.where(lane >= R, lane - R, lane)
        u = jnp.where(lane < rank, total, 0.0).astype(jnp.bfloat16)
        u_ref[span, :] = u
        acc_ref[span, :qcols] += scale * jnp.dot(
            u[:, :R], bq_sel_ref[b], preferred_element_type=jnp.float32
        )
        acc_ref[span, qcols + kcols :] += scale * jnp.dot(
            u[:, R:], bv_sel_ref[b], preferred_element_type=jnp.float32
        )

    @pl.loop(2, n + 1)
    def _(d):
        @pl.when(d < n)
        def _():
            both(d)

        finish(me - d + 1, me - d + 1 >= 0)
        finish(me + d - 1, me + d - 1 < n)

    @pl.loop(1, n)
    def _(j):
        for copy in factor_copies(j, False):
            copy.wait_send()

    for j in range(1, nt):
        part_copy(j, False).wait_send()

    @pl.loop(0, n)
    def _(s):
        for p in range(pieces):

            @pl.when((s <= me) & (me < n - 1))
            def _():
                z_copy(s, p, 0).wait_send()

            @pl.when((s >= me) & (me > 0))
            def _():
                z_copy(s, p, 1).wait_send()

            @pl.when(s != me)
            def _():
                for j in range(1, ng):
                    y_copy(s, p, j, False).wait_send()


def project(tokens, w_query, w_key, w_value, down, b_query, b_value, blocks_of, slots, ranks):
    n, ng, nt = lax.axis_size("dp"), lax.axis_size("groups"), lax.axis_size("tensor")
    rows = tokens.shape[0]
    depth, qcols = w_query.shape
    kcols = w_key.shape[1]
    cols = qcols + 2 * kcols
    half = depth // ng
    pieces = max(1, half // 128)
    blocks = rows // REQUEST_ROWS
    smem = pl.BlockSpec(memory_space=pltpu.SMEM)
    vmem = pl.BlockSpec(memory_space=pltpu.VMEM)
    hbm = pl.BlockSpec(memory_space=pltpu.HBM)
    dma = pltpu.SemaphoreType.DMA
    return pl.pallas_call(
        functools.partial(project_kernel, pieces),
        out_shape=(
            jax.ShapeDtypeStruct((rows, cols), jnp.float32),
            jax.ShapeDtypeStruct((rows, 2 * R), jnp.bfloat16),
            jax.ShapeDtypeStruct((blocks, R, qcols), jnp.bfloat16),
            jax.ShapeDtypeStruct((blocks, R, kcols), jnp.bfloat16),
        ),
        in_specs=[smem] * 3 + [hbm] * 4 + [vmem] * 3,
        out_specs=(vmem,) * 4,
        scratch_shapes=[
            pltpu.VMEM(tokens.shape, jnp.bfloat16),
            pltpu.VMEM((n, depth, cols), jnp.bfloat16),
            pltpu.VMEM((n,) + down.shape, jnp.bfloat16),
            pltpu.VMEM((n,) + b_query.shape, jnp.bfloat16),
            pltpu.VMEM((n,) + b_value.shape, jnp.bfloat16),
            pltpu.VMEM((nt, rows, 2 * R), jnp.float32),
            dma((7,)),
            dma((2, n, pieces)),
            dma((n, pieces)),
            dma((ng, n, pieces)),
            dma((ng, n, pieces)),
            dma((3, n)),
            dma((3, n)),
            dma((nt,)),
            dma((nt,)),
        ],
        compiler_params=pltpu.CompilerParams(
            collective_id=0, has_side_effects=True, vmem_limit_bytes=60 * 1024 * 1024
        ),
        name="project",
    )(blocks_of, slots, ranks, tokens, w_query, w_key, w_value, down, b_query, b_value)


def reduce_kernel(
    block_ref,
    slot_ref,
    rank_ref,
    x_hbm,
    part_ref,
    upq_ref,
    upv_ref,
    low_out,
    upq_out,
    upv_out,
    x_ref,
    back_ref,
    x_sem,
    backs,
    low_send,
    low_got,
    upq_got,
    upv_got,
    b_send,
    b_recv,
    a_send,
    a_recv,
):
    n, nt = lax.axis_size("dp"), lax.axis_size("tensor")
    me, t = lax.axis_index("dp"), lax.axis_index("tensor")
    width = x_ref.shape[1]
    block_count = x_ref.shape[0] // REQUEST_ROWS
    x_copy = pltpu.make_async_copy(
        x_hbm.at[:, pl.ds(pl.multiple_of(t * width, 128), width)], x_ref, x_sem
    )
    x_copy.start()
    greet(("dp", "tensor"))

    def back_copy(j, arriving):
        peer = lax.rem(t + nt - j, nt) if arriving else lax.rem(t + j, nt)
        at = peer if arriving else t
        return pltpu.make_async_remote_copy(
            src_ref=part_ref,
            dst_ref=backs.at[at],
            send_sem=b_send.at[j],
            recv_sem=b_recv.at[j],
            device_id={"tensor": peer},
            device_id_type=MESH,
        )

    def grad_copy(i, src, dst, j, arriving):
        peer = lax.rem(me + n - j, n) if arriving else lax.rem(me + j, n)
        at = peer if arriving else me
        return pltpu.make_async_remote_copy(
            src_ref=src.at[peer],
            dst_ref=dst.at[at],
            send_sem=a_send.at[i, j],
            recv_sem=a_recv.at[i, j],
            device_id={"dp": peer},
            device_id_type=MESH,
        )

    trio = ((0, upq_ref, upq_got), (1, upv_ref, upv_got), (2, low_send, low_got))
    for j in range(1, nt):
        back_copy(j, False).start()

    @pl.loop(1, n)
    def _(j):
        for i, src, dst in trio[:2]:
            grad_copy(i, src, dst, j, False).start()

    backs[t] = part_ref[...]
    for j in range(1, nt):
        back_copy(j, True).wait_recv()
    total = backs[0].astype(jnp.float32)
    for j in range(1, nt):
        total = total + backs[j].astype(jnp.float32)
    lane = lax.broadcasted_iota(jnp.int32, (REQUEST_ROWS, 2 * R), 1)
    lane = jnp.where(lane >= R, lane - R, lane)
    for b in range(block_count):
        span = pl.ds(b * REQUEST_ROWS, REQUEST_ROWS)
        kept = total[b * REQUEST_ROWS : (b + 1) * REQUEST_ROWS]
        back_ref[span, :] = jnp.where(lane < rank_ref[block_ref[b, 0]], kept, 0.0)
    x_copy.wait()

    @pl.loop(1, n + 1)
    def _(j):
        a = lax.rem(me + j, n)
        chosen = jnp.concatenate(
            [
                jnp.where(
                    jnp.full((REQUEST_ROWS, 2 * R), slot_ref[block_ref[b, 0]], jnp.int32) == a,
                    back_ref[pl.ds(b * REQUEST_ROWS, REQUEST_ROWS), :],
                    0.0,
                )
                for b in range(block_count)
            ],
            axis=0,
        ).astype(jnp.bfloat16)
        low_send[a] = lax.dot_general(
            chosen, x_ref[...], (((0,), (0,)), ((), ())), preferred_element_type=jnp.float32
        ).astype(jnp.bfloat16)

        @pl.when(j < n)
        def _():
            grad_copy(2, low_send, low_got, j, False).start()

    low_got[me] = low_send[me]
    upq_got[me] = upq_ref[me]
    upv_got[me] = upv_ref[me]

    for i, src, dst in trio:

        @pl.loop(1, n)
        def _(j):
            grad_copy(i, src, dst, j, True).wait_recv()

    for got, out in ((low_got, low_out), (upq_got, upq_out), (upv_got, upv_out)):
        out[...] = jnp.zeros_like(out)

        @pl.loop(0, n)
        def _(s):
            out[...] += got[s].astype(jnp.float32)

    for j in range(1, nt):
        back_copy(j, False).wait_send()

    for i, src, dst in trio:

        @pl.loop(1, n)
        def _(j):
            grad_copy(i, src, dst, j, False).wait_send()


def reduce_grads(tokens, width, blocks_of, slots, ranks, part, up_q, up_v):
    n, nt = lax.axis_size("dp"), lax.axis_size("tensor")
    rows = tokens.shape[0]
    smem = pl.BlockSpec(memory_space=pltpu.SMEM)
    hbm = pl.BlockSpec(memory_space=pltpu.HBM)
    vmem = pl.BlockSpec(memory_space=pltpu.VMEM)
    dma = pltpu.SemaphoreType.DMA
    low_shape = (n, 2 * R, width)
    return pl.pallas_call(
        reduce_kernel,
        out_shape=(
            jax.ShapeDtypeStruct(low_shape[1:], jnp.float32),
            jax.ShapeDtypeStruct(up_q.shape[1:], jnp.float32),
            jax.ShapeDtypeStruct(up_v.shape[1:], jnp.float32),
        ),
        in_specs=[smem] * 3 + [hbm] + [vmem] * 3,
        out_specs=(vmem,) * 3,
        scratch_shapes=[
            pltpu.VMEM((rows, width), jnp.bfloat16),
            pltpu.VMEM((rows, 2 * R), jnp.float32),
            dma,
            pltpu.VMEM((nt,) + part.shape, jnp.bfloat16),
            pltpu.VMEM(low_shape, jnp.bfloat16),
            pltpu.VMEM(low_shape, jnp.bfloat16),
            pltpu.VMEM(up_q.shape, jnp.bfloat16),
            pltpu.VMEM(up_v.shape, jnp.bfloat16),
            dma((nt,)),
            dma((nt,)),
            dma((3, n)),
            dma((3, n)),
        ],
        compiler_params=pltpu.CompilerParams(
            collective_id=1, has_side_effects=True, vmem_limit_bytes=60 * 1024 * 1024
        ),
        name="reduce_grads",
    )(blocks_of, slots, ranks, tokens, part, up_q, up_v)

def attend_kernel(
    group,
    block_ref,
    slot_ref,
    rank_ref,
    live_ref,
    cos_ref,
    sin_ref,
    q_ref,
    kv_ref,
    u_ref,
    bq_ref,
    bv_ref,
    d_ref,
    part_ref,
    upq_ref,
    upv_ref,
    gq_ref,
    gv_ref,
    upq_sum,
    upv_sum,
):
    b = pl.program_id(0)
    kcols = kv_ref.shape[1] // 2
    kv_heads = kcols // HD
    adapter = block_ref[b, 0]
    slot = slot_ref[adapter]
    scale = scale_of(rank_ref[adapter])
    live = live_ref[0] - b * REQUEST_ROWS

    @pl.when(b == 0)
    def _():
        upq_sum[...] = jnp.zeros_like(upq_sum)
        upv_sum[...] = jnp.zeros_like(upv_sum)

    cosine, sine = cos_ref[...], sin_ref[...]
    dims = (REQUEST_ROWS, REQUEST_ROWS)
    query_at = lax.broadcasted_iota(jnp.int32, dims, 0)
    key_at = lax.broadcasted_iota(jnp.int32, dims, 1)
    allowed = (key_at <= query_at) & ((key_at < live) | (key_at == query_at))
    allowed = jnp.concatenate([allowed.astype(jnp.float32)] * group, axis=0) > 0.5
    live_rows = lax.broadcasted_iota(jnp.int32, (REQUEST_ROWS, HD), 0) < live

    def turn(item, sign):
        return item * cosine + pltpu.roll(item, HD // 2, 1) * (sign * sine)

    def dot(a, c, left, right):
        return lax.dot_general(
            a, c, (((left,), (right,)), ((), ())), preferred_element_type=jnp.float32
        )

    for k in range(kv_heads):
        keys = turn(kv_ref[:, k * HD : (k + 1) * HD], 1.0).astype(jnp.bfloat16)
        values = kv_ref[:, kcols + k * HD : kcols + (k + 1) * HD].astype(jnp.bfloat16)
        heads = [pl.ds((k * group + i) * HD, HD) for i in range(group)]
        queries = jnp.concatenate(
            [turn(q_ref[:, h], 1.0).astype(jnp.bfloat16) for h in heads], axis=0
        )
        dout = jnp.concatenate(
            [
                jnp.where(live_rows, d_ref[:, h].astype(jnp.float32), 0.0).astype(jnp.bfloat16)
                for h in heads
            ],
            axis=0,
        )
        scores = dot(queries, keys, 1, 1) * HD ** (-0.5)
        scores = jnp.where(allowed, scores, -1e30)
        expo = jnp.exp(scores - jnp.max(scores, axis=-1, keepdims=True))
        probs = expo / jnp.sum(expo, axis=-1, keepdims=True)
        dprobs = dot(dout, values, 1, 1)
        dscores = probs * (dprobs - jnp.sum(dprobs * probs, axis=-1, keepdims=True))
        dquery = dot(dscores.astype(jnp.bfloat16), keys, 1, 0) * HD ** (-0.5)
        for i, h in enumerate(heads):
            rows = dquery[i * REQUEST_ROWS : (i + 1) * REQUEST_ROWS]
            gq_ref[:, h] = turn(rows, -1.0).astype(jnp.bfloat16)
        gv_ref[:, k * HD : (k + 1) * HD] = dot(probs.astype(jnp.bfloat16), dout, 0, 0).astype(
            jnp.bfloat16
        )
    u = u_ref[...]
    upq_sum[slot] += scale * dot(u[:, :R], gq_ref[...], 0, 0)
    upv_sum[slot] += scale * dot(u[:, R:], gv_ref[...], 0, 0)
    part_ref[...] = (
        scale
        * jnp.concatenate(
            [dot(gq_ref[...], bq_ref[0], 1, 1), dot(gv_ref[...], bv_ref[0], 1, 1)], axis=-1
        )
    ).astype(jnp.bfloat16)

    @pl.when(b == pl.num_programs(0) - 1)
    def _():
        upq_ref[...] = upq_sum[...].astype(jnp.bfloat16)
        upv_ref[...] = upv_sum[...].astype(jnp.bfloat16)


def attend(full, low_rank, up_query, up_value, d_heads, blocks_of, slots, ranks, live):
    slot_count = slots.shape[0]
    rows, qcols = d_heads.shape
    kcols = up_value.shape[2]
    group = qcols // kcols
    cosine, sine = rope_tables(REQUEST_ROWS, HD)
    cosine = np.concatenate([cosine, cosine], axis=-1)
    sine = np.concatenate([-sine, sine], axis=-1)
    smem = pl.BlockSpec(memory_space=pltpu.SMEM)
    table = pl.BlockSpec((REQUEST_ROWS, HD), lambda b: (0, 0))
    upq_shape = (slot_count, R, qcols)
    upv_shape = (slot_count, R, kcols)
    ratio = qcols // (2 * kcols)
    return pl.pallas_call(
        functools.partial(attend_kernel, group),
        grid=(rows // REQUEST_ROWS,),
        out_shape=(
            jax.ShapeDtypeStruct((rows, 2 * R), jnp.bfloat16),
            jax.ShapeDtypeStruct(upq_shape, jnp.bfloat16),
            jax.ShapeDtypeStruct(upv_shape, jnp.bfloat16),
        ),
        in_specs=[smem] * 4
        + [
            table,
            table,
            pl.BlockSpec((REQUEST_ROWS, qcols), lambda b: (b, 0)),
            pl.BlockSpec((REQUEST_ROWS, 2 * kcols), lambda b: (b, ratio)),
            pl.BlockSpec((REQUEST_ROWS, 2 * R), lambda b: (b, 0)),
            pl.BlockSpec((1, R, qcols), lambda b: (b, 0, 0)),
            pl.BlockSpec((1, R, kcols), lambda b: (b, 0, 0)),
            pl.BlockSpec((REQUEST_ROWS, qcols), lambda b: (b, 0)),
        ],
        out_specs=(
            pl.BlockSpec((REQUEST_ROWS, 2 * R), lambda b: (b, 0)),
            pl.BlockSpec(upq_shape, lambda b: (0, 0, 0)),
            pl.BlockSpec(upv_shape, lambda b: (0, 0, 0)),
        ),
        scratch_shapes=[
            pltpu.VMEM((REQUEST_ROWS, qcols), jnp.bfloat16),
            pltpu.VMEM((REQUEST_ROWS, kcols), jnp.bfloat16),
            pltpu.VMEM(upq_shape, jnp.float32),
            pltpu.VMEM(upv_shape, jnp.float32),
        ],
        name="attend",
    )(
        blocks_of, slots, ranks, live, cosine, sine, full, full, low_rank, up_query, up_value, d_heads
    )


def on_device(
    tokens,
    w_query,
    w_key,
    w_value,
    a_query,
    b_query,
    a_value,
    b_value,
    adapter_ranks,
    adapter_slot,
    block_adapter,
    live_tokens,
    d_heads,
):
    width = a_query.shape[1]
    down = jnp.concatenate([a_query[0].T, a_value[0].T], axis=0)
    full, low_rank, up_query, up_value = project(
        tokens, w_query, w_key, w_value, down, b_query[0], b_value[0],
        block_adapter, adapter_slot, adapter_ranks,
    )
    part, up_q, up_v = attend(
        full, low_rank, up_query, up_value, d_heads,
        block_adapter, adapter_slot, adapter_ranks, live_tokens,
    )
    low, grad_bq, grad_bv = reduce_grads(
        tokens, width, block_adapter, adapter_slot, adapter_ranks, part, up_q, up_v
    )
    return (low[:R].T[None], grad_bq[None], low[R:].T[None], grad_bv[None])


def solution(mesh):
    in_specs = (
        P(("groups", "dp"), None),
        P("dp", "tensor"),
        P("dp", "tensor"),
        P("dp", "tensor"),
        P(("groups", "dp"), "tensor", None),
        P(("groups", "dp"), None, "tensor"),
        P(("groups", "dp"), "tensor", None),
        P(("groups", "dp"), None, "tensor"),
        P("groups"),
        P(),
        P(("groups", "dp"), None),
        P(("groups", "dp")),
        P(("groups", "dp"), "tensor"),
    )
    out_specs = (
        P(("groups", "dp"), "tensor", None),
        P(("groups", "dp"), None, "tensor"),
        P(("groups", "dp"), "tensor", None),
        P(("groups", "dp"), None, "tensor"),
    )
    return jax.shard_map(
        on_device, mesh=mesh, in_specs=in_specs, out_specs=out_specs, check_vma=False
    )
```

profile of v0, /device:TPU:24, one launch (start us, length us, event | category | flops | bytes accessed | tf_op | source)
XLA Modules:
  0.0 179.9 jit_solution(6459886360783930884)
XLA Ops:
  1.3 1.3 copy.21.block_ref
  2.6 1.5 pad_maximum_fusion.down_ref
  4.1 135.2 %project.1 = (f32[512,1536]{1,0:T(8,128)}, bf16[512,64]{1,0:T(8,128)(2,1)}, bf16[4,32,1024]{2,1,0:T(8,128)(2,1)}, bf16[4,32,256]{2,1,0:T(8,128)(2,1)}) custom-call(s32[4,1]{1,0:T(4,128)} %copy.21.block_ref, s32[4]{0:T(128)} %slot_ref.5, s32[4]{0:T(128)} %rank_ref.5, bf16[512,4096]{1,0:T(8,128)(2,1)} %x_hbm.3, bf16[1024,1024]{1,0:T(8,128)(2,1)} %wq_hbm.1, ...), custom_call_target="tpu_custom_call" | custom-call | tf_op jit(solution)/shard_map/project/pallas_call | solution.py:318
  139.4 9.9 %attend.1 = (bf16[512,64]{1,0:T(8,128)(2,1)}, bf16[4,32,1024]{2,1,0:T(8,128)(2,1)}, bf16[4,32,256]{2,1,0:T(8,128)(2,1)}) custom-call(s32[4,1]{1,0:T(4,128)} %copy.21.block_ref, s32[4]{0:T(128)} %slot_ref.5, s32[4]{0:T(128)} %rank_ref.5, s32[1]{0:T(128)S(6)} %copy.24.live_ref, f32[128,128]{1,0:T(8,128)} %constant.4.clone.cos_ref, ...), custom_call_target="tpu_custom_call" | custom-call | tf_op jit(solution)/shard_map/attend/pallas_call | solution.py:626
  149.3 26.0 %reduce_grads.1 = (f32[64,1024]{1,0:T(8,128)}, f32[32,1024]{1,0:T(8,128)}, f32[32,256]{1,0:T(8,128)}) custom-call(s32[4,1]{1,0:T(4,128)} %copy.21.block_ref, s32[4]{0:T(128)} %slot_ref.5, s32[4]{0:T(128)} %rank_ref.5, bf16[512,4096]{1,0:T(8,128)(2,1)} %x_hbm.3, bf16[512,64]{1,0:T(8,128)(2,1)} %get-tuple-element.18.part_ref, ...), custom_call_target="tpu_custom_call" | custom-call | tf_op jit(solution)/shard_map/reduce_grads/pallas_call | solution.py:490
  175.3 1.7 slice_bitcast_fusion
  177.0 1.6 copy.25
  178.5 1.4 copy.26
where the time goes:
time: 182 us; the launch traced here: 180 us
  Pallas kernels  171 us (94%)
  local copies, waits for them, and re-layouts  5.94 us (3%)
    pallas_call x1, Pallas kernels, project(): pl.pallas_call(functools.partial(project_kernel, pieces), out_shape=(jax....  135 us
    pallas_call x1, Pallas kernels, reduce_grads(): pl.pallas_call(reduce_kernel, out_shape=(jax.ShapeDtypeStruct(low_shape[1...  26 us
    pallas_call x1, Pallas kernels, attend(): pl.pallas_call(functools.partial(attend_kernel, group), grid=(rows // REQ...  9.92 us
    unnamed x3, local copies, waits for them, and re-layouts  4.25 us

commit v1 on v0

v1 whole, which is shorter than its diff:
```python
import functools

import jax
import jax.numpy as jnp
import numpy as np
from jax import lax
from jax.experimental import pallas as pl
from jax.experimental.pallas import tpu as pltpu
from jax.sharding import PartitionSpec as P

HD = 128
R = 32
REQUEST_ROWS = 128
MESH = pl.DeviceIdType.MESH

adapter_alpha_factor = 32.0
rope_theta = 500000.0

SUBS = 4
TOKEN_SUBS = 2
FACTORS = 1


def rope_tables(length, width):
    halfway = width // 2
    spread = rope_theta ** (-2.0 * np.arange(halfway, dtype=np.float32) / width)
    angle = np.arange(length, dtype=np.float32)[:, None] * spread.astype(np.float32)[None, :]
    return np.cos(angle).astype(np.float32), np.sin(angle).astype(np.float32)


def scale_of(rank):
    return (adapter_alpha_factor / jnp.full((1, 128), rank, jnp.int32).astype(jnp.float32))[:, :1]


def dot(a, c, left, right):
    return lax.dot_general(
        a, c, (((left,), (right,)), ((), ())), preferred_element_type=jnp.float32
    )


def layer_kernel(
    G,
    block_ref,
    slot_ref,
    rank_ref,
    live_ref,
    x_hbm,
    wq_hbm,
    wk_hbm,
    wv_hbm,
    aq_hbm,
    av_hbm,
    bq_hbm,
    bv_hbm,
    d_hbm,
    cos_ref,
    sin_ref,
    lowq_out,
    lowv_out,
    upq_out,
    upv_out,
    x_all,
    w_kv,
    w_a,
    w_b,
    down_all,
    b_all,
    d_all,
    acc_kv,
    acc_a,
    acc_b,
    parts,
    u_all,
    keys_all,
    values_all,
    gv_acc,
    back_acc,
    upq_sum,
    upv_sum,
    upq_send,
    upv_send,
    upq_got,
    upv_got,
    back_send,
    back_got,
    low_send,
    low_got,
    meta,
    local_sem,
    z_send,
    z_recv,
    yb_send,
    yb_recv,
    yt_send,
    yt_recv,
    tx_send,
    tx_recv,
    tp_send,
    tp_recv,
    part_send,
    part_recv,
    yu_send,
    yu_recv,
    us_send,
    us_recv,
    bk_send,
    bk_recv,
    lo_send,
    lo_recv,
):
    n = lax.axis_size("dp")
    ng = lax.axis_size("groups")
    nt = lax.axis_size("tensor")
    me = lax.axis_index("dp")
    g = lax.axis_index("groups")
    t = lax.axis_index("tensor")
    split = G > 1
    gi = g if split else 0
    rows = x_hbm.shape[0]
    depth, qcols = wq_hbm.shape
    kcols = wk_hbm.shape[1]
    hq, hk = qcols // G, kcols // G
    hc = hq // 2
    kv_heads = hk // HD
    group = hq // hk
    blocks = rows // REQUEST_ROWS
    width = down_all.shape[2]
    step = depth // SUBS
    weights = (w_kv, None, w_a, w_b)
    accs = (acc_kv, None, acc_a, acc_b)

    def at_group(index, **rest):
        if split:
            rest["groups"] = index
        return rest

    def remote(src, dst, send, recv, to):
        return pltpu.make_async_remote_copy(
            src_ref=src, dst_ref=dst, send_sem=send, recv_sem=recv, device_id=to, device_id_type=MESH
        )

    mine = pl.ds(pl.multiple_of(me * depth, depth), depth)
    qs = pl.ds(pl.multiple_of(gi * hq, 128), hq)
    ks = pl.ds(pl.multiple_of(gi * hk, 128), hk)
    loads = [
        (wk_hbm.at[:, ks], w_kv.at[mine, pl.ds(0, hk)]),
        (wv_hbm.at[:, ks], w_kv.at[mine, pl.ds(hk, hk)]),
        (aq_hbm, down_all.at[me, pl.ds(0, R), :]),
        (av_hbm, down_all.at[me, pl.ds(R, R), :]),
        (bq_hbm.at[:, qs], b_all.at[me, gi, :, pl.ds(0, hq)]),
        (bv_hbm.at[:, ks], b_all.at[me, gi, :, pl.ds(hq, hk)]),
        (wq_hbm.at[:, pl.ds(pl.multiple_of(gi * hq, 128), hc)], w_a.at[mine, :]),
        (wq_hbm.at[:, pl.ds(pl.multiple_of(gi * hq + hc, 128), hc)], w_b.at[mine, :]),
        (x_hbm, x_all.at[gi]),
        (d_hbm.at[:, qs], d_all.at[gi]),
    ]
    loads = [pltpu.make_async_copy(s, d, local_sem.at[i]) for i, (s, d) in enumerate(loads)]
    for copy in loads:
        copy.start()

    for b in range(blocks):
        adapter = block_ref[b]
        meta[gi, b] = slot_ref[adapter]
        meta[gi, blocks + b] = rank_ref[adapter]
    meta[gi, 2 * blocks] = live_ref[0]

    barrier = pltpu.get_barrier_semaphore()

    @pl.loop(1, n * G)
    def _(j):
        k = lax.rem(me * G + gi + j, n * G)
        pl.semaphore_signal(
            barrier, inc=1, device_id=at_group(lax.rem(k, G), dp=lax.div(k, G)), device_id_type=MESH
        )

    for j in range(1, nt):
        for e in range(G):
            pl.semaphore_signal(
                barrier,
                inc=1,
                device_id=at_group(lax.rem(gi + e, G), tensor=lax.rem(t + j, nt)),
                device_id_type=MESH,
            )
    pl.semaphore_wait(barrier, n * G - 1 + G * (nt - 1))

    def z_copy(item, s, p, way):
        if item == FACTORS:
            ref = down_all.at[s] if p == 0 else b_all.at[s]
        else:
            ref = weights[item].at[pl.ds(pl.multiple_of(s * depth + p * step, step), step), :]
        target = jnp.clip(me + (1 if way == 0 else -1), 0, n - 1)
        return remote(
            ref, ref, z_send.at[way, item, s, p], z_recv.at[item, s, p], {"dp": target}
        )

    def pieces_of(item):
        return range(2) if item == FACTORS else range(SUBS)

    def send_own(item, pieces=None):
        for p in pieces_of(item) if pieces is None else pieces:

            @pl.when(me < n - 1)
            def _():
                z_copy(item, me, p, 0).start()

            @pl.when(me > 0)
            def _():
                z_copy(item, me, p, 1).start()

    def forward(item, d):
        for p in pieces_of(item):
            for way in (0, 1):
                s = me - d if way == 0 else me + d
                valid = (s >= 0) if way == 0 else (s < n)
                onward = (me < n - 1) if way == 0 else (me > 0)

                @pl.when(valid)
                def _():
                    z_copy(item, s, p, way).wait_recv()

                    @pl.when(onward)
                    def _():
                        z_copy(item, s, p, way).start()

    def line(item, after=None, hooks=()):
        hooks = dict(hooks)
        if n <= 8:
            for d in range(1, n):
                forward(item, d)
                if after is not None:
                    after(d)
                if d in hooks:
                    hooks.pop(d)()
        else:

            @pl.loop(1, n)
            def _(d):
                forward(item, d)
                if after is not None:
                    after(d)

        for hook in hooks.values():
            hook()

    def y_copies(j, arriving):
        peer = lax.rem(gi + G - j, G) if arriving else lax.rem(gi + j, G)
        at = peer if arriving else gi
        to = {"groups": peer}
        pq = pl.ds(pl.multiple_of(peer * hq, 128), hq)
        pk = pl.ds(pl.multiple_of(peer * hk, 128), hk)
        sources = (
            (bq_hbm.at[:, pq], b_all.at[me, at, :, pl.ds(0, hq)]),
            (bv_hbm.at[:, pk], b_all.at[me, at, :, pl.ds(hq, hk)]),
            (meta.at[at], meta.at[at]),
            (d_hbm.at[:, pq], d_all.at[at]),
        )
        return [
            remote(s, d, yb_send.at[j, i], yb_recv.at[j, i], to) for i, (s, d) in enumerate(sources)
        ]

    quarter = rows // nt
    sub = quarter // TOKEN_SUBS

    def token_piece(at, q, k):
        return x_all.at[at, pl.ds(pl.multiple_of(q * quarter + k * sub, sub), sub), :]

    def yt_copy(j, k, arriving):
        peer = lax.rem(gi + G - j, G) if arriving else lax.rem(gi + j, G)
        ref = token_piece(peer if arriving else gi, t, k)
        return remote(ref, ref, yt_send.at[j, k], yt_recv.at[j, k], {"groups": peer})

    pairs = nt // 2
    partner = t + 1 - 2 * lax.rem(t, 2)

    def tx_copy(j, i, k, arriving):
        at = lax.rem(gi + G - j, G)
        peer = lax.rem(t + nt - 2 * i, nt) if arriving else lax.rem(t + 2 * i, nt)
        ref = token_piece(at, peer if arriving else t, k)
        return remote(ref, ref, tx_send.at[j, i, k], tx_recv.at[j, i, k], {"tensor": peer})

    def tp_copy(j, q, k):
        at = lax.rem(gi + G - j, G)
        ref = token_piece(at, q, k)
        return remote(ref, ref, tp_send.at[j, q, k], tp_recv.at[j, q, k], {"tensor": partner})

    def relay_tokens(k):
        for j in range(1, G):
            yt_copy(j, k, True).wait_recv()
            for i in range(1, pairs):
                tx_copy(j, i, k, False).start()
            tp_copy(j, t, k).start()

    def pass_tokens():
        for j in range(1, G):
            for k in range(TOKEN_SUBS):
                for i in range(1, pairs):
                    tx_copy(j, i, k, True).wait_recv()
                    tp_copy(j, lax.rem(t + nt - 2 * i, nt), k).start()

    def settle_tokens():
        for j in range(1, G):
            for k in range(TOKEN_SUBS):
                for i in range(pairs):
                    tp_copy(j, lax.rem(partner + 2 * i, nt), k).wait_recv()

    tile = 256 if rows % 256 == 0 else 128

    def whole_product(item, r):
        @pl.loop(0, rows // tile)
        def _(i):
            span = pl.ds(pl.multiple_of(i * tile, tile), tile)
            accs[item][r, span, :] = jnp.dot(
                x_all[r, span, :], weights[item][...], preferred_element_type=jnp.float32
            )

    def slice_product(item, s, first):
        k_span = pl.ds(pl.multiple_of(s * depth, 128), depth)

        @pl.loop(0, G * rows // tile)
        def _(i):
            r = lax.div(i, rows // tile)
            span = pl.ds(pl.multiple_of(lax.rem(i, rows // tile) * tile, tile), tile)
            new = jnp.dot(
                x_all[r, span, k_span],
                weights[item][k_span, :],
                preferred_element_type=jnp.float32,
            )
            if first:
                accs[item][r, span, :] = new
            else:
                accs[item][r, span, :] += new

    cosine, sine = cos_ref[...], sin_ref[...]
    dims = (REQUEST_ROWS, REQUEST_ROWS)
    query_at = lax.broadcasted_iota(jnp.int32, dims, 0)
    key_at = lax.broadcasted_iota(jnp.int32, dims, 1)

    def turn(item, sign):
        return item * cosine + pltpu.roll(item, HD // 2, 1) * (sign * sine)

    def attend(index, ci):
        r, b = lax.div(index, blocks), lax.rem(index, blocks)
        span = pl.ds(pl.multiple_of(b * REQUEST_ROWS, REQUEST_ROWS), REQUEST_ROWS)
        slot = meta[r, b]
        scale = scale_of(meta[r, blocks + b])
        live = meta[r, 2 * blocks] - b * REQUEST_ROWS
        u = u_all[r, :, span]
        if ci == 0:
            added = scale * dot(u[R:], b_all[slot, r, :, hq:], 0, 0)
            for k in range(kv_heads):
                cs = slice(k * HD, (k + 1) * HD)
                keys_all[r, span, cs] = turn(acc_kv[r, span, cs], 1.0).astype(jnp.bfloat16)
            values_all[r, span, :] = (acc_kv[r, span, hk:] + added).astype(jnp.bfloat16)
        full = accs[2 + ci][r, span, :] + scale * dot(
            u[:R], b_all[slot, r, :, ci * hc : (ci + 1) * hc], 0, 0
        )
        live_rows = lax.broadcasted_iota(jnp.int32, (REQUEST_ROWS, HD), 0) < live
        allowed = (key_at <= query_at) & ((key_at < live) | (key_at == query_at))
        allowed = allowed.astype(jnp.float32)
        pieces = []
        for k in range(kv_heads):
            heads = [i for i in range(hc // HD) if (ci * (hc // HD) + i) // group == k]
            if not heads:
                continue
            kc = slice(k * HD, (k + 1) * HD)
            keys, values = keys_all[r, span, kc], values_all[r, span, kc]
            queries = jnp.concatenate(
                [turn(full[:, i * HD : (i + 1) * HD], 1.0).astype(jnp.bfloat16) for i in heads],
                axis=0,
            )
            dout = jnp.concatenate(
                [
                    jnp.where(
                        live_rows,
                        d_all[r, span, ci * hc + i * HD : ci * hc + (i + 1) * HD].astype(jnp.float32),
                        0.0,
                    ).astype(jnp.bfloat16)
                    for i in heads
                ],
                axis=0,
            )
            mask = jnp.concatenate([allowed] * len(heads), axis=0) > 0.5
            scores = dot(queries, keys, 1, 1) * HD ** (-0.5)
            scores = jnp.where(mask, scores, -1e30)
            expo = jnp.exp(scores - jnp.max(scores, axis=-1, keepdims=True))
            probs = expo / jnp.sum(expo, axis=-1, keepdims=True)
            dprobs = dot(dout, values, 1, 1)
            dscores = probs * (dprobs - jnp.sum(dprobs * probs, axis=-1, keepdims=True))
            dquery = dot(dscores.astype(jnp.bfloat16), keys, 1, 0) * HD ** (-0.5)
            for i in range(len(heads)):
                piece = dquery[i * REQUEST_ROWS : (i + 1) * REQUEST_ROWS]
                pieces.append(turn(piece, -1.0).astype(jnp.bfloat16))
            part_v = dot(probs.astype(jnp.bfloat16), dout, 0, 0)
            if heads[0] + ci * (hc // HD) == k * group:
                gv_acc[r, span, kc] = part_v
            else:
                gv_acc[r, span, kc] += part_v
        gq = jnp.concatenate(pieces, axis=1)
        slots = jnp.full((R, 128), slot, jnp.int32)[:, :1]

        def spread(total, value):
            for a in range(n) if n <= 8 else ():
                total[a] += jnp.where(slots == a, value, 0.0)
            if n > 8:

                @pl.loop(0, n)
                def _(a):
                    total[a] += jnp.where(slots == a, value, 0.0)

        spread(upq_sum.at[ci, r], scale * dot(u[:R], gq, 1, 0))
        back = scale * dot(b_all[slot, r, :, ci * hc : (ci + 1) * hc], gq, 1, 1)
        if ci == 0:
            back_acc[r, :R, span] = back
        else:
            back_acc[r, :R, span] += back
            gv = gv_acc[r, span, :].astype(jnp.bfloat16)
            spread(upv_sum.at[r], scale * dot(u[R:], gv, 1, 0))
            back_acc[r, R:, span] = scale * dot(b_all[slot, r, :, hq:], gv, 1, 1)

    def part_copy(j, arriving):
        peer = lax.rem(t + nt - j, nt) if arriving else lax.rem(t + j, nt)
        ref = parts.at[peer if arriving else t]
        return remote(ref, ref, part_send.at[j], part_recv.at[j], {"tensor": peer})

    def down_parts():
        wide = pl.ds(pl.multiple_of(t * width, 128), width)
        for b in range(blocks):
            span = slice(b * REQUEST_ROWS, (b + 1) * REQUEST_ROWS)
            parts[t, :, span] = dot(down_all[meta[gi, b]], x_all[gi, span, wide], 1, 1)
        for j in range(1, nt):
            part_copy(j, False).start()

    row_at = lax.broadcasted_iota(jnp.int32, (2 * R, REQUEST_ROWS), 0)
    row_at = jnp.where(row_at >= R, row_at - R, row_at)

    def yu_copy(j, arriving):
        peer = lax.rem(gi + G - j, G) if arriving else lax.rem(gi + j, G)
        ref = u_all.at[peer if arriving else gi]
        return remote(ref, ref, yu_send.at[j], yu_recv.at[j], {"groups": peer})

    def finish_down():
        for j in range(1, nt):
            part_copy(j, True).wait_recv()
        for b in range(blocks):
            span = slice(b * REQUEST_ROWS, (b + 1) * REQUEST_ROWS)
            total = parts[0, :, span]
            for j in range(1, nt):
                total = total + parts[j, :, span]
            kept = jnp.where(row_at < meta[gi, blocks + b], total, 0.0)
            u_all[gi, :, span] = kept.astype(jnp.bfloat16)
        for j in range(1, G):
            yu_copy(j, False).start()

    def up_copy(ci, e, a):
        there = lax.rem(gi + e, G)
        src = upv_send.at[there, a] if ci == 2 else upq_send.at[ci, there, a]
        dst = upv_got.at[me, gi] if ci == 2 else upq_got.at[ci, me, gi]
        return remote(
            src, dst, us_send.at[ci, e, a], us_recv.at[ci, me, gi], at_group(there, dp=a)
        )

    def up_arrival(ci, e, s):
        there = lax.rem(gi + e, G)
        dst = upv_got.at[s, there] if ci == 2 else upq_got.at[ci, s, there]
        return remote(dst, dst, us_send.at[ci, e, s], us_recv.at[ci, s, there], at_group(there, dp=s))

    def others(body):
        @pl.loop(0, n)
        def _(a):
            for e in range(G):
                if e == 0:

                    @pl.when(a != me)
                    def _():
                        body(e, a)

                else:
                    body(e, a)

    def send_ups(ci):
        if ci == 2:
            upv_send[...] = upv_sum[...].astype(jnp.bfloat16)
            upv_got[me, gi] = upv_send[gi, me]
        else:
            upq_send[ci] = upq_sum[ci].astype(jnp.bfloat16)
            upq_got[ci, me, gi] = upq_send[ci, gi, me]
        others(lambda e, a: up_copy(ci, e, a).start())

    own_w = (loads[0], loads[1])
    for copy in own_w:
        copy.wait()
    send_own(0)
    for j in range(1, G):
        for copy in y_copies(j, False)[:3]:
            copy.start()
    loads[8].wait()
    for j in range(1, G):
        for k in range(TOKEN_SUBS):
            yt_copy(j, k, False).start()
        y_copies(j, False)[3].start()
    for copy in loads[2:6]:
        copy.wait()
    send_own(FACTORS, (0,))
    for j in range(1, G):
        for copy in y_copies(j, True)[:3]:
            copy.wait_recv()
    send_own(FACTORS, (1,))
    upq_sum[...] = jnp.zeros_like(upq_sum)
    upv_sum[...] = jnp.zeros_like(upv_sum)
    for copy in loads[6:8] + loads[9:]:
        copy.wait()

    relays = [(1 + k, functools.partial(relay_tokens, k)) for k in range(TOKEN_SUBS)]
    line(0, hooks=relays)
    send_own(2)
    line(FACTORS, hooks=[(n - 1, down_parts)])
    pass_tokens()
    send_own(3)
    whole_product(0, gi)

    def tokens_done():
        settle_tokens()
        for j in range(1, G):
            whole_product(0, lax.rem(gi + j, G))

    line(2, hooks=[(1, finish_down), (2, tokens_done)])
    for e in range(G):
        whole_product(2, lax.rem(gi + e, G))
    for j in range(1, G):
        y_copies(j, True)[3].wait_recv()
        yu_copy(j, True).wait_recv()
    slice_product(3, me, True)
    total_blocks = G * blocks
    per = -(-total_blocks // (n - 1)) if n > 1 else total_blocks

    def last_step(d):
        for way in (0, 1):
            s = me - d if way == 0 else me + d

            @pl.when((s >= 0) if way == 0 else (s < n))
            def _():
                slice_product(3, s, False)

        @pl.loop(0, per)
        def _(i):
            index = (d - 1) * per + i

            @pl.when(index < total_blocks)
            def _():
                attend(index, 0)

    line(3, after=last_step)
    send_ups(0)

    @pl.loop(0, total_blocks)
    def _(index):
        attend(index, 1)

    for r in range(G):
        back_send[r] = back_acc[r].astype(jnp.bfloat16)

    def back_copy(e, j, arriving):
        there = lax.rem(gi + e, G)
        peer = lax.rem(t + nt - j, nt) if arriving else lax.rem(t + j, nt)
        if arriving:
            dst = back_got.at[there, peer]
            return remote(
                dst, dst, bk_send.at[e, j], bk_recv.at[there, peer], at_group(there, tensor=peer)
            )
        return remote(
            back_send.at[there],
            back_got.at[gi, t],
            bk_send.at[e, j],
            bk_recv.at[gi, t],
            at_group(there, tensor=peer),
        )

    crossing = [(e, j) for e in range(G) for j in range(nt) if (e, j) != (0, 0)]
    for e, j in crossing:
        back_copy(e, j, False).start()
    send_ups(1)
    send_ups(2)
    back_got[gi, t] = back_send[gi]
    for e, j in crossing:
        back_copy(e, j, True).wait_recv()
    total = jnp.zeros(back_acc.shape[1:], jnp.float32)
    for r in range(G):
        for j in range(nt):
            total = total + back_got[r, j].astype(jnp.float32)
    kept = []
    for b in range(blocks):
        span = slice(b * REQUEST_ROWS, (b + 1) * REQUEST_ROWS)
        kept.append(jnp.where(row_at < meta[gi, blocks + b], total[:, span], 0.0))
    wide = pl.ds(pl.multiple_of(t * width, 128), width)

    def low_copy(a):
        return remote(
            low_send.at[a], low_got.at[me], lo_send.at[a], lo_recv.at[me], {"dp": a}
        )

    stack = 4 if n % 4 == 0 else 1

    @pl.loop(0, n // stack)
    def _(q):
        chosen = jnp.concatenate(
            [
                jnp.concatenate(
                    [
                        jnp.where(
                            jnp.full((2 * R, REQUEST_ROWS), meta[gi, b], jnp.int32) == q * stack + i,
                            kept[b],
                            0.0,
                        )
                        for b in range(blocks)
                    ],
                    axis=1,
                )
                for i in range(stack)
            ],
            axis=0,
        ).astype(jnp.bfloat16)
        low = jnp.dot(chosen, x_all[gi, :, wide], preferred_element_type=jnp.float32)
        for i in range(stack):
            a = q * stack + i
            low_send[a] = low[i * 2 * R : (i + 1) * 2 * R].astype(jnp.bfloat16)

            @pl.when(a != me)
            def _():
                low_copy(a).start()

    low_got[me] = low_send[me]

    for ci in range(3):
        others(lambda e, s: up_arrival(ci, e, s).wait_recv())
    for e in range(G):
        for ci in range(2):
            out = jnp.zeros((R, hc), jnp.float32)
            out = lax.fori_loop(0, n, lambda s, v: v + upq_got[ci, s, e].astype(jnp.float32), out)
            upq_out[:, e * hq + ci * hc : e * hq + (ci + 1) * hc] = out
        out = jnp.zeros((R, hk), jnp.float32)
        out = lax.fori_loop(0, n, lambda s, v: v + upv_got[s, e].astype(jnp.float32), out)
        upv_out[:, e * hk : (e + 1) * hk] = out

    @pl.loop(0, n)
    def _(s):
        @pl.when(s != me)
        def _():
            remote(
                low_got.at[s], low_got.at[s], lo_send.at[s], lo_recv.at[s], {"dp": s}
            ).wait_recv()

    for i, out in enumerate((lowq_out, lowv_out)):
        out[...] = jnp.zeros_like(out)

        @pl.loop(0, n)
        def _(s):
            out[...] += low_got[s, i * R : (i + 1) * R, :].astype(jnp.float32)

    for item in range(4):

        @pl.loop(0, n)
        def _(s):
            for p in pieces_of(item):

                @pl.when((s <= me) & (me < n - 1))
                def _():
                    z_copy(item, s, p, 0).wait_send()

                @pl.when((s >= me) & (me > 0))
                def _():
                    z_copy(item, s, p, 1).wait_send()

    for j in range(1, G):
        for copy in y_copies(j, False):
            copy.wait_send()
        yu_copy(j, False).wait_send()
        for k in range(TOKEN_SUBS):
            yt_copy(j, k, False).wait_send()
            for i in range(1, pairs):
                tx_copy(j, i, k, False).wait_send()
            for i in range(pairs):
                tp_copy(j, lax.rem(t + 2 * i, nt), k).wait_send()
    for j in range(1, nt):
        part_copy(j, False).wait_send()
    for e, j in crossing:
        back_copy(e, j, False).wait_send()
    for ci in range(3):
        others(lambda e, a: up_copy(ci, e, a).wait_send())

    @pl.loop(0, n)
    def _(a):
        @pl.when(a != me)
        def _():
            low_copy(a).wait_send()


def layer(G, x, wq, wk, wv, aq, av, bq, bv, d, blocks_of, slots, ranks, live):
    n, nt = lax.axis_size("dp"), lax.axis_size("tensor")
    rows = x.shape[0]
    depth, qcols = wq.shape
    kcols = wk.shape[1]
    width = aq.shape[1]
    hq, hk = qcols // G, kcols // G
    hc = hq // 2
    span = n * depth
    blocks = rows // REQUEST_ROWS
    cosine, sine = rope_tables(REQUEST_ROWS, HD)
    cosine = np.concatenate([cosine, cosine], axis=-1)
    sine = np.concatenate([-sine, sine], axis=-1)
    smem = pl.BlockSpec(memory_space=pltpu.SMEM)
    vmem = pl.BlockSpec(memory_space=pltpu.VMEM)
    hbm = pl.BlockSpec(memory_space=pltpu.HBM)
    bf, f32 = jnp.bfloat16, jnp.float32
    V = pltpu.VMEM
    dma = pltpu.SemaphoreType.DMA
    return pl.pallas_call(
        functools.partial(layer_kernel, G),
        out_shape=(
            jax.ShapeDtypeStruct((R, width), f32),
            jax.ShapeDtypeStruct((R, width), f32),
            jax.ShapeDtypeStruct((R, qcols), f32),
            jax.ShapeDtypeStruct((R, kcols), f32),
        ),
        in_specs=[smem] * 4 + [hbm] * 9 + [vmem] * 2,
        out_specs=(vmem,) * 4,
        scratch_shapes=[
            V((G, rows, span), bf),
            V((span, 2 * hk), bf),
            V((span, hc), bf),
            V((span, hc), bf),
            V((n, 2 * R, width), bf),
            V((n, G, R, hq + hk), bf),
            V((G, rows, hq), bf),
            V((G, rows, 2 * hk), f32),
            V((G, rows, hc), f32),
            V((G, rows, hc), f32),
            V((nt, 2 * R, rows), f32),
            V((G, 2 * R, rows), bf),
            V((G, rows, hk), bf),
            V((G, rows, hk), bf),
            V((G, rows, hk), f32),
            V((G, 2 * R, rows), f32),
            V((2, G, n, R, hc), f32),
            V((G, n, R, hk), f32),
            V((2, G, n, R, hc), bf),
            V((G, n, R, hk), bf),
            V((2, n, G, R, hc), bf),
            V((n, G, R, hk), bf),
            V((G, 2 * R, rows), bf),
            V((G, nt, 2 * R, rows), bf),
            V((n, 2 * R, width), bf),
            V((n, 2 * R, width), bf),
            pltpu.SMEM((G, 128), jnp.int32),
            dma((10,)),
            dma((2, 4, n, SUBS)),
            dma((4, n, SUBS)),
            dma((G, 4)),
            dma((G, 4)),
            dma((G, TOKEN_SUBS)),
            dma((G, TOKEN_SUBS)),
            dma((G, max(1, nt // 2), TOKEN_SUBS)),
            dma((G, max(1, nt // 2), TOKEN_SUBS)),
            dma((G, nt, TOKEN_SUBS)),
            dma((G, nt, TOKEN_SUBS)),
            dma((nt,)),
            dma((nt,)),
            dma((G,)),
            dma((G,)),
            dma((3, G, n)),
            dma((3, n, G)),
            dma((G, nt)),
            dma((G, nt)),
            dma((n,)),
            dma((n,)),
        ],
        compiler_params=pltpu.CompilerParams(
            collective_id=0, has_side_effects=True, vmem_limit_bytes=62 * 1024 * 1024
        ),
        name="layer",
    )(blocks_of, slots, ranks, live, x, wq, wk, wv, aq, av, bq, bv, d, cosine, sine)


def on_device(
    tokens,
    w_query,
    w_key,
    w_value,
    a_query,
    b_query,
    a_value,
    b_value,
    adapter_ranks,
    adapter_slot,
    block_adapter,
    live_tokens,
    d_heads,
):
    ng, nt = lax.axis_size("groups"), lax.axis_size("tensor")
    kv_heads = w_key.shape[1] // HD
    G = ng if nt % 2 == 0 and kv_heads % ng == 0 else 1
    low_q, low_v, up_q, up_v = layer(
        G, tokens, w_query, w_key, w_value, a_query[0].T, a_value[0].T, b_query[0], b_value[0],
        d_heads, block_adapter.reshape(-1), adapter_slot, adapter_ranks, live_tokens,
    )
    return low_q.T[None], up_q[None], low_v.T[None], up_v[None]


def solution(mesh):
    in_specs = (
        P(("groups", "dp"), None),
        P("dp", "tensor"),
        P("dp", "tensor"),
        P("dp", "tensor"),
        P(("groups", "dp"), "tensor", None),
        P(("groups", "dp"), None, "tensor"),
        P(("groups", "dp"), "tensor", None),
        P(("groups", "dp"), None, "tensor"),
        P("groups"),
        P(),
        P(("groups", "dp"), None),
        P(("groups", "dp")),
        P(("groups", "dp"), "tensor"),
    )
    out_specs = (
        P(("groups", "dp"), "tensor", None),
        P(("groups", "dp"), None, "tensor"),
        P(("groups", "dp"), "tensor", None),
        P(("groups", "dp"), None, "tensor"),
    )
    return jax.shard_map(
        on_device, mesh=mesh, in_specs=in_specs, out_specs=out_specs, check_vma=False
    )
```

time: 182 us -> 167 us (0.918)
  Pallas kernels: 171 us -> 159 us
    pallas_call x3 -> x1, Pallas kernels: 171 us -> 159 us  [layer(): pl.pallas_call(functools.partial(layer_kernel, G), out_shape=(jax.ShapeDt...]
    unnamed x3 -> x4, local copies, waits for them, and re-layouts: 4.25 us -> 6.08 us
where the time goes in v1:
time: 167 us; the launch traced here: 166 us
  Pallas kernels  159 us (95%)
  local copies, waits for them, and re-layouts  6.08 us (4%)
    pallas_call x1, Pallas kernels, layer(): pl.pallas_call(functools.partial(layer_kernel, G), out_shape=(jax.ShapeDt...  159 us
    unnamed x4, local copies, waits for them, and re-layouts  6.08 us

profile of v1, /device:TPU:24, one launch (start us, length us, event | category | flops | bytes accessed | tf_op | source)
XLA Modules:
  0.0 166.1 jit_solution(16758147358888636568)
XLA Ops:
  1.3 158.7 %layer.1 = (f32[32,1024]{1,0:T(8,128)}, f32[32,1024]{1,0:T(8,128)}, f32[32,1024]{1,0:T(8,128)}, f32[32,256]{1,0:T(8,128)}) custom-call(s32[4]{0:T(128)} %bitcast.25, s32[4]{0:T(128)} %slot_ref.1, s32[4]{0:T(128)} %rank_ref.1, s32[1]{0:T(128)S(6)} %copy.23.live_ref, bf16[512,4096]{1,0:T(8,128)(2,1)} %x_hbm.1, bf16[1024,1024]{1,0:T(8,128)(2,1)} %wq_hbm.1, ...), custom_call_target="tpu_custom_call" | custom-call | tf_op jit(solution)/shard_map/layer/pallas_call | solution.py:716
  160.0 1.6 copy.24
  161.6 1.6 copy.25
  163.1 1.6 copy.26
  164.7 1.4 copy.27

commit v2 on v1

v2 whole, which is shorter than its diff:
```python
import functools

import jax
import jax.numpy as jnp
import numpy as np
from jax import lax
from jax.experimental import pallas as pl
from jax.experimental.pallas import tpu as pltpu
from jax.sharding import PartitionSpec as P

HD = 128
R = 32
REQUEST_ROWS = 128
MESH = pl.DeviceIdType.MESH

adapter_alpha_factor = 32.0
rope_theta = 500000.0

SUBS = 4
TOKEN_SUBS = 2
FACTORS = 1


def rope_tables(length, width):
    halfway = width // 2
    spread = rope_theta ** (-2.0 * np.arange(halfway, dtype=np.float32) / width)
    angle = np.arange(length, dtype=np.float32)[:, None] * spread.astype(np.float32)[None, :]
    return np.cos(angle).astype(np.float32), np.sin(angle).astype(np.float32)


def scale_of(rank):
    return (adapter_alpha_factor / jnp.full((1, 128), rank, jnp.int32).astype(jnp.float32))[:, :1]


def dot(a, c, left, right):
    return lax.dot_general(
        a, c, (((left,), (right,)), ((), ())), preferred_element_type=jnp.float32
    )


def layer_kernel(
    G,
    relief,
    block_ref,
    slot_ref,
    rank_ref,
    live_ref,
    x_hbm,
    wq_hbm,
    wk_hbm,
    wv_hbm,
    aq_hbm,
    av_hbm,
    bq_hbm,
    bv_hbm,
    d_hbm,
    cos_ref,
    sin_ref,
    lowq_out,
    lowv_out,
    upq_out,
    upv_out,
    x_all,
    w_kv,
    w_a,
    w_b,
    down_all,
    b_all,
    d_all,
    acc_kv,
    acc_a,
    acc_b,
    parts,
    u_all,
    keys_all,
    values_all,
    gv_acc,
    back_acc,
    upq_sum,
    upv_sum,
    upq_send,
    upv_send,
    upq_got,
    upv_got,
    back_send,
    back_got,
    low_send,
    low_got,
    meta,
    x_far,
    x_down,
    parts_extra,
    p_b_send,
    p_a_send,
    p_b_got,
    p_a_got,
    local_sem,
    z_send,
    z_recv,
    yb_send,
    yb_recv,
    yt_send,
    yt_recv,
    tx_send,
    tx_recv,
    tp_send,
    tp_recv,
    part_send,
    part_recv,
    yu_send,
    yu_recv,
    us_send,
    us_recv,
    bk_send,
    bk_recv,
    lo_send,
    lo_recv,
    em_send,
    em_recv,
    et_send,
    et_recv,
    ey_send,
    ey_recv,
    eu_send,
    eu_recv,
    px_send,
    px_recv,
    ue_send,
    ue_recv,
    pp_send,
    pp_recv,
):
    n = lax.axis_size("dp")
    ng = lax.axis_size("groups")
    nt = lax.axis_size("tensor")
    me = lax.axis_index("dp")
    g = lax.axis_index("groups")
    t = lax.axis_index("tensor")
    split = G > 1
    low_end, high_end = (1, n - 2) if relief else (0, n - 1)
    end = (me < low_end) | (me > high_end)
    near = ((me == 1) | (me == n - 2)) if relief else None
    inward = jnp.where(me == 0, 1, n - 2) if relief else None
    outward = jnp.where(me == 1, 0, n - 1) if relief else None
    gi = g if split else 0
    rows = x_hbm.shape[0]
    depth, qcols = wq_hbm.shape
    kcols = wk_hbm.shape[1]
    hq, hk = qcols // G, kcols // G
    hc = hq // 2
    kv_heads = hk // HD
    group = hq // hk
    blocks = rows // REQUEST_ROWS
    width = down_all.shape[2]
    step = depth // SUBS
    weights = (w_kv, None, w_a, w_b)
    wide = pl.ds(pl.multiple_of(t * width, 128), width)
    accs = (acc_kv, None, acc_a, acc_b)
    sums_out, sums_in = {2: p_a_send, 3: p_b_send}, {2: p_a_got, 3: p_b_got}
    far = x_far.shape[2]
    far_of_near = jnp.where(me == 1, 2 * depth, 0)
    far_of_end = jnp.where(me == 0, 2 * depth, 0)
    close_of_end = jnp.where(me == 0, 0, far)

    def at_group(index, **rest):
        if split:
            rest["groups"] = index
        return rest

    def remote(src, dst, send, recv, to):
        return pltpu.make_async_remote_copy(
            src_ref=src, dst_ref=dst, send_sem=send, recv_sem=recv, device_id=to, device_id_type=MESH
        )

    mine = pl.ds(pl.multiple_of(me * depth, depth), depth)
    qs = pl.ds(pl.multiple_of(gi * hq, 128), hq)
    ks = pl.ds(pl.multiple_of(gi * hk, 128), hk)
    loads = [
        (wk_hbm.at[:, ks], w_kv.at[mine, pl.ds(0, hk)]),
        (wv_hbm.at[:, ks], w_kv.at[mine, pl.ds(hk, hk)]),
        (aq_hbm, down_all.at[me, pl.ds(0, R), :]),
        (av_hbm, down_all.at[me, pl.ds(R, R), :]),
        (bq_hbm.at[:, qs], b_all.at[me, gi, :, pl.ds(0, hq)]),
        (bv_hbm.at[:, ks], b_all.at[me, gi, :, pl.ds(hq, hk)]),
        (wq_hbm.at[:, pl.ds(pl.multiple_of(gi * hq, 128), hc)], w_a.at[mine, :]),
        (wq_hbm.at[:, pl.ds(pl.multiple_of(gi * hq + hc, 128), hc)], w_b.at[mine, :]),
        (x_hbm, x_all.at[gi]),
        (d_hbm.at[:, qs], d_all.at[gi]),
    ]
    loads = [pltpu.make_async_copy(s, d, local_sem.at[i]) for i, (s, d) in enumerate(loads)]
    for copy in loads:
        copy.start()

    for b in range(blocks):
        adapter = block_ref[b]
        meta[gi, b] = slot_ref[adapter]
        meta[gi, blocks + b] = rank_ref[adapter]
    meta[gi, 2 * blocks] = live_ref[0]

    with jax.named_scope("greet"):
        barrier = pltpu.get_barrier_semaphore()

        @pl.loop(1, n * G)
        def _(j):
            k = lax.rem(me * G + gi + j, n * G)
            pl.semaphore_signal(
                barrier, inc=1, device_id=at_group(lax.rem(k, G), dp=lax.div(k, G)), device_id_type=MESH
            )

        for j in range(1, nt):
            for e in range(G):
                pl.semaphore_signal(
                    barrier,
                    inc=1,
                    device_id=at_group(lax.rem(gi + e, G), tensor=lax.rem(t + j, nt)),
                    device_id_type=MESH,
                )
        pl.semaphore_wait(barrier, n * G - 1 + G * (nt - 1))

    def z_copy(item, s, p, way):
        if item == FACTORS:
            ref = down_all.at[s] if p == 0 else b_all.at[s]
        else:
            ref = weights[item].at[pl.ds(pl.multiple_of(s * depth + p * step, step), step), :]
        target = jnp.clip(me + (1 if way == 0 else -1), 0, n - 1)
        return remote(
            ref, ref, z_send.at[way, item, s, p], z_recv.at[item, s, p], {"dp": target}
        )

    def pieces_of(item):
        return range(2) if item == FACTORS else range(SUBS)

    def stays_inside(item, p, own):
        if item == FACTORS:
            return p == 0
        return item > FACTORS and not own

    def ups(item, p, own):
        return me < (high_end if stays_inside(item, p, own) else n - 1)

    def downs(item, p, own):
        return me > (low_end if stays_inside(item, p, own) else 0)

    def send_own(item, pieces=None, to_end=None):
        up, down = (me < n, me >= 0) if to_end is None else (me == n - 2, me == 1)
        if to_end is False:
            up, down = ~up, ~down
        for p in pieces_of(item) if pieces is None else pieces:

            @pl.when(ups(item, p, True) & up)
            def _():
                z_copy(item, me, p, 0).start()

            @pl.when(downs(item, p, True) & down)
            def _():
                z_copy(item, me, p, 1).start()

    def forward_piece(item, d, p, static_p):
        for way in (0, 1):
            s = me - d if way == 0 else me + d
            valid = (s >= 0) if way == 0 else (s < n)
            if relief and stays_inside(item, static_p, False):
                valid = valid & (~end if item == FACTORS else ~end | (d == 1))
            onward = ups(item, static_p, False) if way == 0 else downs(item, static_p, False)

            @pl.when(valid)
            def _():
                z_copy(item, s, p, way).wait_recv()

                @pl.when(onward)
                def _():
                    z_copy(item, s, p, way).start()

    def line(item, hooks=()):
        hooks = dict(hooks)
        last = pieces_of(item)[-1]
        if n <= 8:
            for d in range(1, n):
                for p in pieces_of(item):
                    forward_piece(item, d, p, p)
                    for key in ((d, p), (d, None) if p == last else None):
                        if key in hooks:
                            hooks.pop(key)()
        else:

            @pl.loop(1, n)
            def _(d):
                for p in pieces_of(item):
                    forward_piece(item, d, p, p)

        for hook in hooks.values():
            hook()

    def y_copies(j, arriving):
        peer = lax.rem(gi + G - j, G) if arriving else lax.rem(gi + j, G)
        at = peer if arriving else gi
        to = {"groups": peer}
        pq = pl.ds(pl.multiple_of(peer * hq, 128), hq)
        pk = pl.ds(pl.multiple_of(peer * hk, 128), hk)
        sources = (
            (bq_hbm.at[:, pq], b_all.at[me, at, :, pl.ds(0, hq)]),
            (bv_hbm.at[:, pk], b_all.at[me, at, :, pl.ds(hq, hk)]),
            (meta.at[at], meta.at[at]),
            (d_hbm.at[:, pq], d_all.at[at]),
        )
        return [
            remote(s, d, yb_send.at[j, i], yb_recv.at[j, i], to) for i, (s, d) in enumerate(sources)
        ]

    quarter = rows // nt
    sub = quarter // TOKEN_SUBS

    def token_piece(r, q, k, bank=0):
        ref = x_far if bank else x_all
        return ref.at[r, pl.ds(pl.multiple_of(q * quarter + k * sub, sub), sub), :]

    def yt_copy(j, k, arriving):
        peer = lax.rem(gi + G - j, G) if arriving else lax.rem(gi + j, G)
        ref = token_piece(peer if arriving else gi, t, k)
        return remote(ref, ref, yt_send.at[j, k], yt_recv.at[j, k], {"groups": peer})

    pairs = nt // 2
    partner = t + 1 - 2 * lax.rem(t, 2)

    def tx_copy(r, i, k, arriving, bank=0):
        peer = lax.rem(t + nt - 2 * i, nt) if arriving else lax.rem(t + 2 * i, nt)
        ref = token_piece(r, peer if arriving else t, k, bank)
        return remote(
            ref, ref, tx_send.at[bank * G + r, i, k], tx_recv.at[bank * G + r, i, k], {"tensor": peer}
        )

    def tp_copy(r, q, k, bank=0):
        ref = token_piece(r, q, k, bank)
        return remote(
            ref, ref, tp_send.at[bank * G + r, q, k], tp_recv.at[bank * G + r, q, k], {"tensor": partner}
        )

    def spread_tokens(r, k, bank=0):
        for i in range(1, pairs):
            tx_copy(r, i, k, False, bank).start()
        tp_copy(r, t, k, bank).start()

    def pass_tokens(r, bank=0):
        for k in range(TOKEN_SUBS):
            for i in range(1, pairs):
                tx_copy(r, i, k, True, bank).wait_recv()
                tp_copy(r, lax.rem(t + nt - 2 * i, nt), k, bank).start()

    def settle_tokens(r, bank=0):
        for k in range(TOKEN_SUBS):
            for i in range(pairs):
                tp_copy(r, lax.rem(partner + 2 * i, nt), k, bank).wait_recv()

    def drain_tokens(r, bank=0):
        for k in range(TOKEN_SUBS):
            for i in range(1, pairs):
                tx_copy(r, i, k, False, bank).wait_send()
            for i in range(pairs):
                tp_copy(r, lax.rem(t + 2 * i, nt), k, bank).wait_send()

    def relay_tokens(k):
        for j in range(1, G):
            yt_copy(j, k, True).wait_recv()
            spread_tokens(lax.rem(gi + G - j, G), k)

    def end_meta():
        return remote(meta.at[gi], meta.at[G], em_send, em_recv, {"dp": inward})

    def end_tokens(k):
        at = pl.ds(pl.multiple_of(t * quarter + k * sub, sub), sub)
        cols = pl.ds(pl.multiple_of(far_of_end, 128), far)
        return remote(
            x_all.at[gi, at, cols], token_piece(gi, t, k, 1), et_send.at[k], et_recv.at[k], {"dp": inward}
        )

    def end_down():
        return remote(x_all.at[gi, :, wide], x_down, eu_send, eu_recv, {"dp": inward})

    def ey_copy(j, k, arriving):
        peer = lax.rem(gi + G - j, G) if arriving else lax.rem(gi + j, G)
        ref = token_piece(peer if arriving else gi, t, k, 1)
        return remote(ref, ref, ey_send.at[j, k], ey_recv.at[j, k], {"groups": peer})

    def px_copy(j, arriving):
        peer = lax.rem(t + nt - j, nt) if arriving else lax.rem(t + j, nt)
        ref = parts_extra.at[peer if arriving else t]
        return remote(ref, ref, px_send.at[j], px_recv.at[j], {"tensor": peer})

    def ue_copy():
        return remote(u_all.at[G], u_all.at[gi], ue_send, ue_recv, {"dp": outward})

    def pp_copy(item, r):
        i = item - 2
        return remote(
            sums_out[item].at[r], sums_in[item].at[r], pp_send.at[i, r], pp_recv.at[i, r], {"dp": outward}
        )

    tile = 256 if rows % 256 == 0 else 128

    def whole_product(item, r):
        @pl.loop(0, rows // tile)
        def _(i):
            span = pl.ds(pl.multiple_of(i * tile, tile), tile)
            accs[item][r, span, :] = jnp.dot(
                x_all[r, span, :], weights[item][...], preferred_element_type=jnp.float32
            )

    def far_sums(item, r):
        rows_far = pl.ds(pl.multiple_of(far_of_near, 128), far)

        @pl.loop(0, rows // tile)
        def _(i):
            span = pl.ds(pl.multiple_of(i * tile, tile), tile)
            sums_out[item][r, span, :] = jnp.dot(
                x_far[r, span, :], weights[item][rows_far, :], preferred_element_type=jnp.float32
            ).astype(jnp.bfloat16)

        pp_copy(item, r).start()

    def close_product(item, r):
        close = pl.ds(pl.multiple_of(close_of_end, 128), 2 * depth)
        remote(
            sums_in[item].at[r], sums_in[item].at[r], pp_send.at[item - 2, r], pp_recv.at[item - 2, r],
            {"dp": inward},
        ).wait_recv()

        @pl.loop(0, rows // tile)
        def _(i):
            span = pl.ds(pl.multiple_of(i * tile, tile), tile)
            accs[item][r, span, :] = jnp.dot(
                x_all[r, span, close], weights[item][close, :], preferred_element_type=jnp.float32
            ) + sums_in[item][r, span, :].astype(jnp.float32)

    def slice_product(item, s, first):
        k_span = pl.ds(pl.multiple_of(s * depth, 128), depth)

        @pl.loop(0, G * rows // tile)
        def _(i):
            r = lax.div(i, rows // tile)
            span = pl.ds(pl.multiple_of(lax.rem(i, rows // tile) * tile, tile), tile)
            new = jnp.dot(
                x_all[r, span, k_span],
                weights[item][k_span, :],
                preferred_element_type=jnp.float32,
            )
            if first:
                accs[item][r, span, :] = new
            else:
                accs[item][r, span, :] += new

    cosine, sine = cos_ref[...], sin_ref[...]
    dims = (REQUEST_ROWS, REQUEST_ROWS)
    query_at = lax.broadcasted_iota(jnp.int32, dims, 0)
    key_at = lax.broadcasted_iota(jnp.int32, dims, 1)

    def turn(item, sign):
        return item * cosine + pltpu.roll(item, HD // 2, 1) * (sign * sine)

    def place(index):
        r, b = lax.div(index, blocks), lax.rem(index, blocks)
        span = pl.ds(pl.multiple_of(b * REQUEST_ROWS, REQUEST_ROWS), REQUEST_ROWS)
        return r, b, span

    def spread(total, slot, value):
        slots = jnp.full((R, 128), slot, jnp.int32)[:, :1]

        def add(a):
            total[a] += jnp.where(slots == a, value, 0.0)

        if n <= 8:
            for a in range(n):
                add(a)
        else:
            pl.loop(0, n)(add)

    def prepare(index):
        r, b, span = place(index)
        scale = scale_of(meta[r, blocks + b])
        added = scale * dot(u_all[r, R:, span], b_all[meta[r, b], r, :, hq:], 0, 0)
        for k in range(kv_heads):
            cs = slice(k * HD, (k + 1) * HD)
            keys_all[r, span, cs] = turn(acc_kv[r, span, cs], 1.0).astype(jnp.bfloat16)
        values_all[r, span, :] = (acc_kv[r, span, hk:] + added).astype(jnp.bfloat16)
        gv_acc[r, span, :] = jnp.zeros((REQUEST_ROWS, hk), jnp.float32)
        back_acc[r, :, span] = jnp.zeros((2 * R, REQUEST_ROWS), jnp.float32)

    def finish_values(index):
        r, b, span = place(index)
        slot = meta[r, b]
        scale = scale_of(meta[r, blocks + b])
        gv = gv_acc[r, span, :].astype(jnp.bfloat16)
        spread(upv_sum.at[r], slot, scale * dot(u_all[r, R:, span], gv, 1, 0))
        back_acc[r, R:, span] = scale * dot(b_all[slot, r, :, hq:], gv, 1, 1)

    def attend(index, ci):
        r, b, span = place(index)
        slot = meta[r, b]
        scale = scale_of(meta[r, blocks + b])
        live = meta[r, 2 * blocks] - b * REQUEST_ROWS
        u = u_all[r, :R, span]
        b_cols = b_all[slot, r, :, ci * hc : (ci + 1) * hc]
        full = accs[2 + ci][r, span, :] + scale * dot(u, b_cols, 0, 0)
        live_rows = lax.broadcasted_iota(jnp.int32, (REQUEST_ROWS, HD), 0) < live
        allowed = (key_at <= query_at) & ((key_at < live) | (key_at == query_at))
        allowed = allowed.astype(jnp.float32)
        pieces = []
        for k in range(kv_heads):
            heads = [i for i in range(hc // HD) if (ci * (hc // HD) + i) // group == k]
            if not heads:
                continue
            kc = slice(k * HD, (k + 1) * HD)
            keys, values = keys_all[r, span, kc], values_all[r, span, kc]
            queries = jnp.concatenate(
                [turn(full[:, i * HD : (i + 1) * HD], 1.0).astype(jnp.bfloat16) for i in heads],
                axis=0,
            )
            douts = []
            for i in heads:
                rows_in = d_all[r, span, ci * hc + i * HD : ci * hc + (i + 1) * HD]
                kept = jnp.where(live_rows, rows_in.astype(jnp.float32), 0.0)
                douts.append(kept.astype(jnp.bfloat16))
            dout = jnp.concatenate(douts, axis=0)
            mask = jnp.concatenate([allowed] * len(heads), axis=0) > 0.5
            scores = dot(queries, keys, 1, 1) * HD ** (-0.5)
            scores = jnp.where(mask, scores, -1e30)
            expo = jnp.exp(scores - jnp.max(scores, axis=-1, keepdims=True))
            probs = expo / jnp.sum(expo, axis=-1, keepdims=True)
            dprobs = dot(dout, values, 1, 1)
            dscores = probs * (dprobs - jnp.sum(dprobs * probs, axis=-1, keepdims=True))
            dquery = dot(dscores.astype(jnp.bfloat16), keys, 1, 0) * HD ** (-0.5)
            for i in range(len(heads)):
                piece = dquery[i * REQUEST_ROWS : (i + 1) * REQUEST_ROWS]
                pieces.append(turn(piece, -1.0).astype(jnp.bfloat16))
            gv_acc[r, span, kc] += dot(probs.astype(jnp.bfloat16), dout, 0, 0)
        gq = jnp.concatenate(pieces, axis=1)
        spread(upq_sum.at[ci, r], slot, scale * dot(u, gq, 1, 0))
        back_acc[r, :R, span] += scale * dot(b_cols, gq, 1, 1)

    def part_copy(j, arriving):
        peer = lax.rem(t + nt - j, nt) if arriving else lax.rem(t + j, nt)
        ref = parts.at[peer if arriving else t]
        return remote(ref, ref, part_send.at[j], part_recv.at[j], {"tensor": peer})

    def down_product(r, x_ref, into):
        for b in range(blocks):
            span = slice(b * REQUEST_ROWS, (b + 1) * REQUEST_ROWS)
            into[t, :, span] = dot(down_all[meta[r, b]], x_ref[span, :], 1, 1)

    def down_sum(r, terms):
        for b in range(blocks):
            span = slice(b * REQUEST_ROWS, (b + 1) * REQUEST_ROWS)
            total = terms[0, :, span]
            for j in range(1, nt):
                total = total + terms[j, :, span]
            kept = jnp.where(row_at < meta[r, blocks + b], total, 0.0)
            u_all[r, :, span] = kept.astype(jnp.bfloat16)

    def down_parts():
        @pl.when(~end)
        def _():
            down_product(gi, x_all.at[gi, :, wide], parts)
            for j in range(1, nt):
                part_copy(j, False).start()

    row_at = lax.broadcasted_iota(jnp.int32, (2 * R, REQUEST_ROWS), 0)
    row_at = jnp.where(row_at >= R, row_at - R, row_at)

    def yu_copy(j, arriving):
        peer = lax.rem(gi + G - j, G) if arriving else lax.rem(gi + j, G)
        ref = u_all.at[peer if arriving else gi]
        return remote(ref, ref, yu_send.at[j], yu_recv.at[j], {"groups": peer})

    def finish_down():
        @pl.when(~end)
        def _():
            for j in range(1, nt):
                part_copy(j, True).wait_recv()
            down_sum(gi, parts)

        if relief:

            @pl.when(end)
            def _():
                ue_copy().wait_recv()

        for j in range(1, G):
            yu_copy(j, False).start()

    def up_copy(ci, e, a):
        there = lax.rem(gi + e, G)
        src = upv_send.at[there, a] if ci == 2 else upq_send.at[ci, there, a]
        dst = upv_got.at[me, gi] if ci == 2 else upq_got.at[ci, me, gi]
        return remote(
            src, dst, us_send.at[ci, e, a], us_recv.at[ci, me, gi], at_group(there, dp=a)
        )

    def up_arrival(ci, e, s):
        there = lax.rem(gi + e, G)
        dst = upv_got.at[s, there] if ci == 2 else upq_got.at[ci, s, there]
        return remote(dst, dst, us_send.at[ci, e, s], us_recv.at[ci, s, there], at_group(there, dp=s))

    def others(body):
        @pl.loop(0, n)
        def _(a):
            for e in range(G):
                if e == 0:

                    @pl.when(a != me)
                    def _():
                        body(e, a)

                else:
                    body(e, a)

    def send_ups(ci):
        if ci == 2:
            upv_send[...] = upv_sum[...].astype(jnp.bfloat16)
            upv_got[me, gi] = upv_send[gi, me]
        else:
            upq_send[ci] = upq_sum[ci].astype(jnp.bfloat16)
            upq_got[ci, me, gi] = upq_send[ci, gi, me]
        others(lambda e, a: up_copy(ci, e, a).start())

    with jax.named_scope("start"):
        own_w = (loads[0], loads[1])
        for copy in own_w:
            copy.wait()
        send_own(0)
        for j in range(1, G):
            for copy in y_copies(j, False)[:3]:
                copy.start()
        if relief:

            @pl.when(end)
            def _():
                end_meta().start()

        loads[8].wait()
        for j in range(1, G):
            for k in range(TOKEN_SUBS):
                yt_copy(j, k, False).start()
            y_copies(j, False)[3].start()
        for copy in loads[2:6]:
            copy.wait()
        send_own(FACTORS, (0,))
        for j in range(1, G):
            for copy in y_copies(j, True)[:3]:
                copy.wait_recv()
        send_own(FACTORS, (1,))
        for copy in loads[6:8]:
            copy.wait()
        if relief:

            @pl.when(end)
            def _():
                for k in range(TOKEN_SUBS):
                    end_tokens(k).start()

        if relief:

            @pl.when(end)
            def _():
                send_own(2)
                end_down().start()
                send_own(3)

        upq_sum[...] = jnp.zeros_like(upq_sum)
        upv_sum[...] = jnp.zeros_like(upv_sum)
        loads[9].wait()
    other_planes = [lax.rem(gi + j, G) for j in range(1, G)]
    with jax.named_scope("line0"):
        keys_of = [(1, None), (2, 1)]
        line(0, hooks=[(keys_of[k], functools.partial(relay_tokens, k)) for k in range(TOKEN_SUBS)])

        @pl.when(~end)
        def _():
            send_own(2)

    if relief:
        with jax.named_scope("relay_extra"):

            @pl.when(near)
            def _():
                remote(meta.at[G], meta.at[G], em_send, em_recv, {"dp": outward}).wait_recv()
                for k in range(TOKEN_SUBS):
                    et = token_piece(gi, t, k, 1)
                    remote(et, et, et_send.at[k], et_recv.at[k], {"dp": outward}).wait_recv()
                    for j in range(1, G):
                        ey_copy(j, k, False).start()
                    spread_tokens(gi, k, 1)

    with jax.named_scope("pass"):
        for r in other_planes:
            pass_tokens(r)
    with jax.named_scope("linef"):
        line(FACTORS, hooks=[((n - 1, None), down_parts)])
        if relief:

            @pl.when(near)
            def _():
                send_own(3, to_end=True)


    def extra_pass():
        if relief:

            @pl.when(near)
            def _():
                pass_tokens(gi, 1)
                for j in range(1, G):
                    for k in range(TOKEN_SUBS):
                        ey_copy(j, k, True).wait_recv()
                        spread_tokens(lax.rem(gi + G - j, G), k, 1)

        whole_product(0, gi)

    def tokens_done():
        for r in other_planes:
            settle_tokens(r)
            whole_product(0, r)

        @pl.when(~end)
        def _():
            finish_down()

    with jax.named_scope("line2"):
        line(2, hooks=[((1, None), extra_pass), ((2, None), tokens_done)])

        @pl.when(~end)
        def _():
            send_own(3, to_end=False if relief else None)

    if relief:
        with jax.named_scope("far_sums"):

            @pl.when(near)
            def _():
                settle_tokens(gi, 1)
                far_sums(2, gi)

    with jax.named_scope("whole2"):

        @pl.when(~end)
        def _():
            for e in range(G):
                whole_product(2, lax.rem(gi + e, G))
            for j in range(1, G):
                yu_copy(j, True).wait_recv()

            slice_product(3, me, True)

        for j in range(1, G):
            y_copies(j, True)[3].wait_recv()
    total_blocks = G * blocks
    steps = (n - 1) * SUBS
    per = -(-total_blocks // SUBS)
    per_end = -(-total_blocks // (2 * SUBS))

    def first_unit(k):
        index = lax.rem(gi + lax.div(k, blocks), G) * blocks + lax.rem(k, blocks)
        prepare(index)
        attend(index, 0)

    def near_step(i):
        @pl.when(i == 0)
        def _():
            remote(x_down, x_down, eu_send, eu_recv, {"dp": outward}).wait_recv()
            down_product(G, x_down, parts_extra)
            for j in range(1, nt):
                px_copy(j, False).start()
            for r in other_planes:
                pass_tokens(r, 1)

        @pl.when(i == 1)
        def _():
            for j in range(1, nt):
                px_copy(j, True).wait_recv()
            down_sum(G, parts_extra)
            ue_copy().start()

        @pl.when(i == 2)
        def _():
            for r in other_planes:
                settle_tokens(r, 1)
                far_sums(2, r)

    def end_step(i):
        @pl.when(i == SUBS)
        def _():
            finish_down()
            close_product(2, gi)

        @pl.when(i == 2 * SUBS)
        def _():
            for r in other_planes:
                close_product(2, r)
            for j in range(1, G):
                yu_copy(j, True).wait_recv()

    with jax.named_scope("line3"):

        @pl.loop(0, steps)
        def _(i):
            d, p = lax.div(i, SUBS) + 1, lax.rem(i, SUBS)
            forward_piece(3, d, p, 0)

            @pl.when(p == SUBS - 1)
            def _():
                for way in (0, 1):
                    s = me - d if way == 0 else me + d

                    @pl.when(((s >= 0) if way == 0 else (s < n)) & ~end)
                    def _():
                        slice_product(3, s, False)

            if relief:
                pl.when(near)(lambda: near_step(i))
                pl.when(end)(lambda: end_step(i))
                start = jnp.where(end, (i - SUBS) * per_end, i * per)
                count = jnp.where(end, per_end, per)
            else:
                start, count = i * per, per

            @pl.loop(0, max(per, per_end))
            def _(j):
                @pl.when((j < count) & (start + j >= 0) & (start + j < total_blocks))
                def _():
                    first_unit(start + j)

        if not steps:
            pl.loop(0, total_blocks)(first_unit)
    with jax.named_scope("tail_attend"):
        if relief:

            @pl.when(near)
            def _():
                for e in range(G):
                    far_sums(3, lax.rem(gi + e, G))

        send_ups(0)

        @pl.loop(0, G)
        def _(e):
            r = lax.rem(gi + e, G)
            if relief:

                @pl.when(end)
                def _():
                    close_product(3, r)

            @pl.loop(0, blocks)
            def _(b):
                attend(r * blocks + b, 1)
                finish_values(r * blocks + b)

    with jax.named_scope("back"):
        for r in range(G):
            back_send[r] = back_acc[r].astype(jnp.bfloat16)

    def back_copy(e, j, arriving):
        there = lax.rem(gi + e, G)
        peer = lax.rem(t + nt - j, nt) if arriving else lax.rem(t + j, nt)
        if arriving:
            dst = back_got.at[there, peer]
            return remote(
                dst, dst, bk_send.at[e, j], bk_recv.at[there, peer], at_group(there, tensor=peer)
            )
        return remote(
            back_send.at[there],
            back_got.at[gi, t],
            bk_send.at[e, j],
            bk_recv.at[gi, t],
            at_group(there, tensor=peer),
        )

    crossing = [(e, j) for e in range(G) for j in range(nt) if (e, j) != (0, 0)]
    with jax.named_scope("backx"):
        for e, j in crossing:
            back_copy(e, j, False).start()
        send_ups(1)
        send_ups(2)
        back_got[gi, t] = back_send[gi]
        for e, j in crossing:
            back_copy(e, j, True).wait_recv()
    total = jnp.zeros(back_acc.shape[1:], jnp.float32)
    for r in range(G):
        for j in range(nt):
            total = total + back_got[r, j].astype(jnp.float32)
    kept = []
    for b in range(blocks):
        span = slice(b * REQUEST_ROWS, (b + 1) * REQUEST_ROWS)
        kept.append(jnp.where(row_at < meta[gi, blocks + b], total[:, span], 0.0))
    def low_copy(a):
        return remote(
            low_send.at[a], low_got.at[me], lo_send.at[a], lo_recv.at[me], {"dp": a}
        )

    stack = 4 if n % 4 == 0 else 1

    with jax.named_scope("low"):
        @pl.loop(0, n // stack)
        def _(q):
            chosen = jnp.concatenate(
                [
                    jnp.concatenate(
                        [
                            jnp.where(
                                jnp.full((2 * R, REQUEST_ROWS), meta[gi, b], jnp.int32) == q * stack + i,
                                kept[b],
                                0.0,
                            )
                            for b in range(blocks)
                        ],
                        axis=1,
                    )
                    for i in range(stack)
                ],
                axis=0,
            ).astype(jnp.bfloat16)
            low = jnp.dot(chosen, x_all[gi, :, wide], preferred_element_type=jnp.float32)
            for i in range(stack):
                a = q * stack + i
                low_send[a] = low[i * 2 * R : (i + 1) * 2 * R].astype(jnp.bfloat16)

                @pl.when(a != me)
                def _():
                    low_copy(a).start()

        low_got[me] = low_send[me]

    with jax.named_scope("upsum"):
        for ci in range(3):
            others(lambda e, s: up_arrival(ci, e, s).wait_recv())
        for e in range(G):
            for ci in range(2):
                out = jnp.zeros((R, hc), jnp.float32)
                out = lax.fori_loop(0, n, lambda s, v: v + upq_got[ci, s, e].astype(jnp.float32), out)
                upq_out[:, e * hq + ci * hc : e * hq + (ci + 1) * hc] = out
            out = jnp.zeros((R, hk), jnp.float32)
            out = lax.fori_loop(0, n, lambda s, v: v + upv_got[s, e].astype(jnp.float32), out)
            upv_out[:, e * hk : (e + 1) * hk] = out

    with jax.named_scope("lowx"):
        @pl.loop(0, n)
        def _(s):
            @pl.when(s != me)
            def _():
                remote(
                    low_got.at[s], low_got.at[s], lo_send.at[s], lo_recv.at[s], {"dp": s}
                ).wait_recv()

        for i, out in enumerate((lowq_out, lowv_out)):
            out[...] = jnp.zeros_like(out)

            @pl.loop(0, n)
            def _(s):
                out[...] += low_got[s, i * R : (i + 1) * R, :].astype(jnp.float32)

    with jax.named_scope("drain"):
        for item in range(4):

            @pl.loop(0, n)
            def _(s):
                for p in pieces_of(item):

                    for own in (True, False):

                        @pl.when(((s == me) if own else (s < me)) & ups(item, p, own))
                        def _():
                            z_copy(item, s, p, 0).wait_send()

                        @pl.when(((s == me) if own else (s > me)) & downs(item, p, own))
                        def _():
                            z_copy(item, s, p, 1).wait_send()

        for j in range(1, G):
            for copy in y_copies(j, False):
                copy.wait_send()
            yu_copy(j, False).wait_send()
            for k in range(TOKEN_SUBS):
                yt_copy(j, k, False).wait_send()
        for r in other_planes:
            drain_tokens(r)
        if relief:

            @pl.when(end)
            def _():
                end_meta().wait_send()
                end_down().wait_send()
                for k in range(TOKEN_SUBS):
                    end_tokens(k).wait_send()

            @pl.when(near)
            def _():
                for j in range(1, G):
                    for k in range(TOKEN_SUBS):
                        ey_copy(j, k, False).wait_send()
                for e in range(G):
                    drain_tokens(e, 1)
                    pp_copy(2, e).wait_send()
                    pp_copy(3, e).wait_send()
                for j in range(1, nt):
                    px_copy(j, False).wait_send()
                ue_copy().wait_send()

        @pl.when(~end)
        def _():
            for j in range(1, nt):
                part_copy(j, False).wait_send()

        for e, j in crossing:
            back_copy(e, j, False).wait_send()
        for ci in range(3):
            others(lambda e, a: up_copy(ci, e, a).wait_send())

        @pl.loop(0, n)
        def _(a):
            @pl.when(a != me)
            def _():
                low_copy(a).wait_send()


def layer(G, relief, x, wq, wk, wv, aq, av, bq, bv, d, blocks_of, slots, ranks, live):
    n, nt = lax.axis_size("dp"), lax.axis_size("tensor")
    rows = x.shape[0]
    depth, qcols = wq.shape
    kcols = wk.shape[1]
    width = aq.shape[1]
    hq, hk = qcols // G, kcols // G
    hc = hq // 2
    span = n * depth
    blocks = rows // REQUEST_ROWS
    far = (n - 2) * depth
    cosine, sine = rope_tables(REQUEST_ROWS, HD)
    cosine = np.concatenate([cosine, cosine], axis=-1)
    sine = np.concatenate([-sine, sine], axis=-1)
    smem = pl.BlockSpec(memory_space=pltpu.SMEM)
    vmem = pl.BlockSpec(memory_space=pltpu.VMEM)
    hbm = pl.BlockSpec(memory_space=pltpu.HBM)
    bf, f32 = jnp.bfloat16, jnp.float32
    V = pltpu.VMEM
    dma = pltpu.SemaphoreType.DMA

    def pairs_of(shape):
        return [dma(shape), dma(shape)]

    return pl.pallas_call(
        functools.partial(layer_kernel, G, relief),
        out_shape=(
            jax.ShapeDtypeStruct((R, width), f32),
            jax.ShapeDtypeStruct((R, width), f32),
            jax.ShapeDtypeStruct((R, qcols), f32),
            jax.ShapeDtypeStruct((R, kcols), f32),
        ),
        in_specs=[smem] * 4 + [hbm] * 9 + [vmem] * 2,
        out_specs=(vmem,) * 4,
        scratch_shapes=[
            V((G, rows, span), bf),
            V((span, 2 * hk), bf),
            V((span, hc), bf),
            V((span, hc), bf),
            V((n, 2 * R, width), bf),
            V((n, G, R, hq + hk), bf),
            V((G, rows, hq), bf),
            V((G, rows, 2 * hk), f32),
            V((G, rows, hc), f32),
            V((G, rows, hc), f32),
            V((nt, 2 * R, rows), f32),
            V((G + 1, 2 * R, rows), bf),
            V((G, rows, hk), bf),
            V((G, rows, hk), bf),
            V((G, rows, hk), f32),
            V((G, 2 * R, rows), f32),
            V((2, G, n, R, hc), f32),
            V((G, n, R, hk), f32),
            V((2, G, n, R, hc), bf),
            V((G, n, R, hk), bf),
            V((2, n, G, R, hc), bf),
            V((n, G, R, hk), bf),
            V((G, 2 * R, rows), bf),
            V((G, nt, 2 * R, rows), bf),
            V((n, 2 * R, width), bf),
            V((n, 2 * R, width), bf),
            pltpu.SMEM((G + 1, 128), jnp.int32),
            V((G, rows, far) if relief else (1, 16, 128), bf),
            V((rows, width) if relief else (16, 128), bf),
            V((nt, 2 * R, rows) if relief else (1, 8, 128), f32),
            V((G, rows, hc) if relief else (1, 16, 128), bf),
            V((G, rows, hc) if relief else (1, 16, 128), bf),
            V((G, rows, hc) if relief else (1, 16, 128), bf),
            V((G, rows, hc) if relief else (1, 16, 128), bf),
        ]
        + pairs_of((10,))[:1]
        + [dma((2, 4, n, SUBS)), dma((4, n, SUBS))]
        + pairs_of((G, 4))
        + pairs_of((G, TOKEN_SUBS))
        + pairs_of((2 * G, max(1, nt // 2), TOKEN_SUBS))
        + pairs_of((2 * G, nt, TOKEN_SUBS))
        + pairs_of((nt,))
        + pairs_of((G,))
        + [dma((3, G, n)), dma((3, n, G))]
        + pairs_of((G, nt))
        + pairs_of((n,))
        + [dma, dma]
        + pairs_of((TOKEN_SUBS,))
        + pairs_of((G, TOKEN_SUBS))
        + [dma, dma]
        + pairs_of((nt,))
        + [dma, dma]
        + pairs_of((2, G)),
        compiler_params=pltpu.CompilerParams(
            collective_id=0, has_side_effects=True, vmem_limit_bytes=62 * 1024 * 1024
        ),
        name="layer",
    )(blocks_of, slots, ranks, live, x, wq, wk, wv, aq, av, bq, bv, d, cosine, sine)


def on_device(
    tokens,
    w_query,
    w_key,
    w_value,
    a_query,
    b_query,
    a_value,
    b_value,
    adapter_ranks,
    adapter_slot,
    block_adapter,
    live_tokens,
    d_heads,
):
    ng, nt = lax.axis_size("groups"), lax.axis_size("tensor")
    kv_heads = w_key.shape[1] // HD
    G = ng if nt % 2 == 0 and kv_heads % ng == 0 else 1
    relief = G > 1 and lax.axis_size("dp") >= 4
    low_q, low_v, up_q, up_v = layer(
        G, relief, tokens, w_query, w_key, w_value, a_query[0].T, a_value[0].T, b_query[0], b_value[0],
        d_heads, block_adapter.reshape(-1), adapter_slot, adapter_ranks, live_tokens,
    )
    return low_q.T[None], up_q[None], low_v.T[None], up_v[None]


def solution(mesh):
    in_specs = (
        P(("groups", "dp"), None),
        P("dp", "tensor"),
        P("dp", "tensor"),
        P("dp", "tensor"),
        P(("groups", "dp"), "tensor", None),
        P(("groups", "dp"), None, "tensor"),
        P(("groups", "dp"), "tensor", None),
        P(("groups", "dp"), None, "tensor"),
        P("groups"),
        P(),
        P(("groups", "dp"), None),
        P(("groups", "dp")),
        P(("groups", "dp"), "tensor"),
    )
    out_specs = (
        P(("groups", "dp"), "tensor", None),
        P(("groups", "dp"), None, "tensor"),
        P(("groups", "dp"), "tensor", None),
        P(("groups", "dp"), None, "tensor"),
    )
    return jax.shard_map(
        on_device, mesh=mesh, in_specs=in_specs, out_specs=out_specs, check_vma=False
    )
```

time: 167 us -> 142 us (0.85)
  Pallas kernels: 159 us -> 133 us
    pallas_call x1, Pallas kernels: 159 us -> 133 us  [layer(): pl.pallas_call(functools.partial(layer_kernel, G, relief), out_shape=(jax...]
where the time goes in v2:
time: 142 us; the launch traced here: 140 us
  Pallas kernels  133 us (94%)
  local copies, waits for them, and re-layouts  6.08 us (4%)
    pallas_call x1, Pallas kernels, layer(): pl.pallas_call(functools.partial(layer_kernel, G, relief), out_shape=(jax...  133 us
    unnamed x4, local copies, waits for them, and re-layouts  6.08 us

profile of v2, /device:TPU:24, one launch (start us, length us, event | category | flops | bytes accessed | tf_op | source)
XLA Modules:
  0.0 140.5 jit_solution(10350108988680972839)
XLA Ops:
  1.3 133.1 %layer.1 = (f32[32,1024]{1,0:T(8,128)}, f32[32,1024]{1,0:T(8,128)}, f32[32,1024]{1,0:T(8,128)}, f32[32,256]{1,0:T(8,128)}) custom-call(s32[4]{0:T(128)} %bitcast.25, s32[4]{0:T(128)} %slot_ref.1, s32[4]{0:T(128)} %rank_ref.1, s32[1]{0:T(128)S(6)} %copy.23.live_ref, bf16[512,4096]{1,0:T(8,128)(2,1)} %x_hbm.1, bf16[1024,1024]{1,0:T(8,128)(2,1)} %wq_hbm.1, ...), custom_call_target="tpu_custom_call" | custom-call | tf_op jit(solution)/shard_map/layer/pallas_call | solution.py:1047
  134.4 1.6 %copy.24 = f32[1,1024,32]{1,2,0:T(8,128)} copy(f32[1,1024,32]{1,2,0:T(8,128)} %bitcast.19) | data formatting | bytes 262144
  136.0 1.6 %copy.25 = f32[1,32,1024]{2,1,0:T(8,128)} copy(f32[1,32,1024]{2,1,0:T(8,128)} %bitcast.18) | data formatting | bytes 262144
  137.5 1.6 %copy.26 = f32[1,1024,32]{1,2,0:T(8,128)} copy(f32[1,1024,32]{1,2,0:T(8,128)} %bitcast.17) | data formatting | bytes 262144
  139.1 1.4 copy.27

commit v3 on v2

--- a/solution.py
+++ b/solution.py
@@ -30,6 +30,11 @@
 
 def scale_of(rank):
     return (adapter_alpha_factor / jnp.full((1, 128), rank, jnp.int32).astype(jnp.float32))[:, :1]
+
+
+def query_chunks(heads):
+    quarter = heads // 4
+    return [heads - 2 * quarter, quarter, quarter] if quarter else [heads]
 
 
 def dot(a, c, left, right):
@@ -56,20 +61,15 @@
     d_hbm,
     cos_ref,
     sin_ref,
-    lowq_out,
-    lowv_out,
-    upq_out,
-    upv_out,
+    out_ref,
     x_all,
     w_kv,
-    w_a,
-    w_b,
+    w_q,
     down_all,
     b_all,
     d_all,
     acc_kv,
-    acc_a,
-    acc_b,
+    acc_q,
     parts,
     u_all,
     keys_all,
@@ -90,10 +90,8 @@
     x_far,
     x_down,
     parts_extra,
-    p_b_send,
-    p_a_send,
-    p_b_got,
-    p_a_got,
+    p_send,
+    p_got,
     local_sem,
     z_send,
     z_recv,
@@ -147,16 +145,17 @@
     depth, qcols = wq_hbm.shape
     kcols = wk_hbm.shape[1]
     hq, hk = qcols // G, kcols // G
-    hc = hq // 2
     kv_heads = hk // HD
     group = hq // hk
     blocks = rows // REQUEST_ROWS
     width = down_all.shape[2]
     step = depth // SUBS
-    weights = (w_kv, None, w_a, w_b)
+    widths = [c * HD for c in query_chunks(hq // HD)]
+    starts = [sum(widths[:i]) for i in range(len(widths))]
+    last = len(widths) - 1
+    weights = (w_kv, None) + tuple(w_q)
     wide = pl.ds(pl.multiple_of(t * width, 128), width)
-    accs = (acc_kv, None, acc_a, acc_b)
-    sums_out, sums_in = {2: p_a_send, 3: p_b_send}, {2: p_a_got, 3: p_b_got}
+    accs = (acc_kv, None) + tuple(acc_q)
     far = x_far.shape[2]
     far_of_near = jnp.where(me == 1, 2 * depth, 0)
     far_of_end = jnp.where(me == 0, 2 * depth, 0)
@@ -182,10 +181,11 @@
         (av_hbm, down_all.at[me, pl.ds(R, R), :]),
         (bq_hbm.at[:, qs], b_all.at[me, gi, :, pl.ds(0, hq)]),
         (bv_hbm.at[:, ks], b_all.at[me, gi, :, pl.ds(hq, hk)]),
-        (wq_hbm.at[:, pl.ds(pl.multiple_of(gi * hq, 128), hc)], w_a.at[mine, :]),
-        (wq_hbm.at[:, pl.ds(pl.multiple_of(gi * hq + hc, 128), hc)], w_b.at[mine, :]),
         (x_hbm, x_all.at[gi]),
         (d_hbm.at[:, qs], d_all.at[gi]),
+    ] + [
+        (wq_hbm.at[:, pl.ds(pl.multiple_of(gi * hq + c, 128), w)], ref.at[mine, :])
+        for c, w, ref in zip(starts, widths, w_q)
     ]
     loads = [pltpu.make_async_copy(s, d, local_sem.at[i]) for i, (s, d) in enumerate(loads)]
     for copy in loads:
@@ -262,6 +262,8 @@
             if relief and stays_inside(item, static_p, False):
                 valid = valid & (~end if item == FACTORS else ~end | (d == 1))
             onward = ups(item, static_p, False) if way == 0 else downs(item, static_p, False)
+            if relief and item > 2:
+                valid = valid & ~(near & (d == 1) & ((s == 0) | (s == n - 1)))
 
             @pl.when(valid)
             def _():
@@ -271,14 +273,26 @@
                 def _():
                     z_copy(item, s, p, way).start()
 
-    def line(item, hooks=()):
+    def forward_ends(item):
+        for way, at in ((0, 1), (1, n - 2)):
+            s = 0 if way == 0 else n - 1
+
+            @pl.when(me == at)
+            def _():
+                for p in pieces_of(item):
+                    z_copy(item, s, p, way).wait_recv()
+                    z_copy(item, s, p, way).start()
+
+    def line(item, after=None, hooks=()):
         hooks = dict(hooks)
-        last = pieces_of(item)[-1]
+        final = pieces_of(item)[-1]
         if n <= 8:
             for d in range(1, n):
                 for p in pieces_of(item):
                     forward_piece(item, d, p, p)
-                    for key in ((d, p), (d, None) if p == last else None):
+                    if p == final and after is not None:
+                        after(d)
+                    for key in ((d, p), (d, None) if p == final else None):
                         if key in hooks:
                             hooks.pop(key)()
         else:
@@ -287,6 +301,8 @@
             def _(d):
                 for p in pieces_of(item):
                     forward_piece(item, d, p, p)
+                if after is not None:
+                    after(d)
 
         for hook in hooks.values():
             hook()
@@ -392,7 +408,7 @@
     def pp_copy(item, r):
         i = item - 2
         return remote(
-            sums_out[item].at[r], sums_in[item].at[r], pp_send.at[i, r], pp_recv.at[i, r], {"dp": outward}
+            p_send[item - 2].at[r], p_got[item - 2].at[r], pp_send.at[i, r], pp_recv.at[i, r], {"dp": outward}
         )
 
     tile = 256 if rows % 256 == 0 else 128
@@ -411,7 +427,7 @@
         @pl.loop(0, rows // tile)
         def _(i):
             span = pl.ds(pl.multiple_of(i * tile, tile), tile)
-            sums_out[item][r, span, :] = jnp.dot(
+            p_send[item - 2][r, span, :] = jnp.dot(
                 x_far[r, span, :], weights[item][rows_far, :], preferred_element_type=jnp.float32
             ).astype(jnp.bfloat16)
 
@@ -420,7 +436,7 @@
     def close_product(item, r):
         close = pl.ds(pl.multiple_of(close_of_end, 128), 2 * depth)
         remote(
-            sums_in[item].at[r], sums_in[item].at[r], pp_send.at[item - 2, r], pp_recv.at[item - 2, r],
+            p_got[item - 2].at[r], p_got[item - 2].at[r], pp_send.at[item - 2, r], pp_recv.at[item - 2, r],
             {"dp": inward},
         ).wait_recv()
 
@@ -429,7 +445,7 @@
             span = pl.ds(pl.multiple_of(i * tile, tile), tile)
             accs[item][r, span, :] = jnp.dot(
                 x_all[r, span, close], weights[item][close, :], preferred_element_type=jnp.float32
-            ) + sums_in[item][r, span, :].astype(jnp.float32)
+            ) + p_got[item - 2][r, span, :].astype(jnp.float32)
 
     def slice_product(item, s, first):
         k_span = pl.ds(pl.multiple_of(s * depth, 128), depth)
@@ -456,11 +472,6 @@
     def turn(item, sign):
         return item * cosine + pltpu.roll(item, HD // 2, 1) * (sign * sine)
 
-    def place(index):
-        r, b = lax.div(index, blocks), lax.rem(index, blocks)
-        span = pl.ds(pl.multiple_of(b * REQUEST_ROWS, REQUEST_ROWS), REQUEST_ROWS)
-        return r, b, span
-
     def spread(total, slot, value):
         slots = jnp.full((R, 128), slot, jnp.int32)[:, :1]
 
@@ -473,68 +484,130 @@
         else:
             pl.loop(0, n)(add)
 
-    def prepare(index):
-        r, b, span = place(index)
-        scale = scale_of(meta[r, blocks + b])
-        added = scale * dot(u_all[r, R:, span], b_all[meta[r, b], r, :, hq:], 0, 0)
-        for k in range(kv_heads):
-            cs = slice(k * HD, (k + 1) * HD)
-            keys_all[r, span, cs] = turn(acc_kv[r, span, cs], 1.0).astype(jnp.bfloat16)
-        values_all[r, span, :] = (acc_kv[r, span, hk:] + added).astype(jnp.bfloat16)
-        gv_acc[r, span, :] = jnp.zeros((REQUEST_ROWS, hk), jnp.float32)
-        back_acc[r, :, span] = jnp.zeros((2 * R, REQUEST_ROWS), jnp.float32)
-
-    def finish_values(index):
-        r, b, span = place(index)
-        slot = meta[r, b]
-        scale = scale_of(meta[r, blocks + b])
-        gv = gv_acc[r, span, :].astype(jnp.bfloat16)
-        spread(upv_sum.at[r], slot, scale * dot(u_all[r, R:, span], gv, 1, 0))
-        back_acc[r, R:, span] = scale * dot(b_all[slot, r, :, hq:], gv, 1, 1)
-
-    def attend(index, ci):
-        r, b, span = place(index)
+    def attend(r, b, ci):
+        span = pl.ds(pl.multiple_of(b * REQUEST_ROWS, REQUEST_ROWS), REQUEST_ROWS)
         slot = meta[r, b]
         scale = scale_of(meta[r, blocks + b])
         live = meta[r, 2 * blocks] - b * REQUEST_ROWS
-        u = u_all[r, :R, span]
-        b_cols = b_all[slot, r, :, ci * hc : (ci + 1) * hc]
-        full = accs[2 + ci][r, span, :] + scale * dot(u, b_cols, 0, 0)
+        u_q, u_v = u_all[r, :R, span], u_all[r, R:, span]
+        b_cols = b_all[slot, r, :, starts[ci] : starts[ci] + widths[ci]]
+        b_v = b_all[slot, r, :, hq:]
+        stores = []
+        heads_of = [slice(k * HD, (k + 1) * HD) for k in range(kv_heads)]
+        if ci == 0:
+            values = (acc_kv[r, span, hk:] + scale * dot(u_v, b_v, 0, 0)).astype(jnp.bfloat16)
+            keys = [turn(acc_kv[r, span, kc], 1.0).astype(jnp.bfloat16) for kc in heads_of]
+            keys = jnp.concatenate(keys, axis=1)
+            yield
+
+            def store_kv():
+                keys_all[r, span, :] = keys
+                values_all[r, span, :] = values
+
+            if last:
+                stores.append(store_kv)
+            gv = [jnp.zeros((REQUEST_ROWS, HD), jnp.float32) for _ in heads_of]
+            back = 0.0
+        else:
+            keys, values = keys_all[r, span, :], values_all[r, span, :]
+            gv = [gv_acc[r, span, kc] for kc in heads_of]
+            back = back_acc[r, :R, span]
+        added = dot(u_q, b_cols, 0, 0)
+        yield
+        full = acc_q[ci][r, span, :] + scale * added
         live_rows = lax.broadcasted_iota(jnp.int32, (REQUEST_ROWS, HD), 0) < live
         allowed = (key_at <= query_at) & ((key_at < live) | (key_at == query_at))
         allowed = allowed.astype(jnp.float32)
         pieces = []
+        first = starts[ci] // HD
         for k in range(kv_heads):
-            heads = [i for i in range(hc // HD) if (ci * (hc // HD) + i) // group == k]
+            heads = [i for i in range(widths[ci] // HD) if (first + i) // group == k]
             if not heads:
                 continue
-            kc = slice(k * HD, (k + 1) * HD)
-            keys, values = keys_all[r, span, kc], values_all[r, span, kc]
+            head_keys, head_values = keys[:, heads_of[k]], values[:, heads_of[k]]
             queries = jnp.concatenate(
                 [turn(full[:, i * HD : (i + 1) * HD], 1.0).astype(jnp.bfloat16) for i in heads],
                 axis=0,
             )
             douts = []
             for i in heads:
-                rows_in = d_all[r, span, ci * hc + i * HD : ci * hc + (i + 1) * HD]
+                rows_in = d_all[r, span, (first + i) * HD : (first + i + 1) * HD]
                 kept = jnp.where(live_rows, rows_in.astype(jnp.float32), 0.0)
                 douts.append(kept.astype(jnp.bfloat16))
             dout = jnp.concatenate(douts, axis=0)
+            yield
+            scores = dot(queries, head_keys, 1, 1)
+            dprobs = dot(dout, head_values, 1, 1)
+            yield
             mask = jnp.concatenate([allowed] * len(heads), axis=0) > 0.5
-            scores = dot(queries, keys, 1, 1) * HD ** (-0.5)
-            scores = jnp.where(mask, scores, -1e30)
-            expo = jnp.exp(scores - jnp.max(scores, axis=-1, keepdims=True))
-            probs = expo / jnp.sum(expo, axis=-1, keepdims=True)
-            dprobs = dot(dout, values, 1, 1)
-            dscores = probs * (dprobs - jnp.sum(dprobs * probs, axis=-1, keepdims=True))
-            dquery = dot(dscores.astype(jnp.bfloat16), keys, 1, 0) * HD ** (-0.5)
+            scores = jnp.where(mask, scores * HD ** (-0.5), -1e30)
+            top = jnp.max(scores, axis=-1, keepdims=True)
+            yield
+            expo = jnp.exp(scores - top)
+            total = jnp.sum(expo, axis=-1, keepdims=True)
+            yield
+            probs = expo / total
+            mean = jnp.sum(dprobs * probs, axis=-1, keepdims=True)
+            yield
+            dscores = (probs * (dprobs - mean)).astype(jnp.bfloat16)
+            dquery = dot(dscores, head_keys, 1, 0)
+            gv[k] = gv[k] + dot(probs.astype(jnp.bfloat16), dout, 0, 0)
+            yield
+            dquery = dquery * HD ** (-0.5)
             for i in range(len(heads)):
                 piece = dquery[i * REQUEST_ROWS : (i + 1) * REQUEST_ROWS]
                 pieces.append(turn(piece, -1.0).astype(jnp.bfloat16))
-            gv_acc[r, span, kc] += dot(probs.astype(jnp.bfloat16), dout, 0, 0)
+            yield
         gq = jnp.concatenate(pieces, axis=1)
-        spread(upq_sum.at[ci, r], slot, scale * dot(u, gq, 1, 0))
-        back_acc[r, :R, span] += scale * dot(b_cols, gq, 1, 1)
+        up = dot(u_q, gq, 1, 0)
+        back_new = dot(b_cols, gq, 1, 1)
+        gv = jnp.concatenate(gv, axis=1)
+        if ci == last:
+            gv = gv.astype(jnp.bfloat16)
+            up_v = dot(u_v, gv, 1, 0)
+            back_v = dot(b_v, gv, 1, 1)
+        yield
+        up = scale * up
+        back = back + scale * back_new
+        if ci == last:
+            up_v, back_v = scale * up_v, scale * back_v
+
+        def store():
+            back_acc[r, :R, span] = back
+            spread(upq_sum[ci].at[r], slot, up)
+            if ci == last:
+                back_acc[r, R:, span] = back_v
+                spread(upv_sum.at[r], slot, up_v)
+            else:
+                gv_acc[r, span, :] = gv
+
+        yield stores + [store]
+
+    together = 4 if blocks % 4 == 0 else 1
+
+    def attend_chunk(ci):
+        @pl.loop(0, G)
+        def _(e):
+            r = lax.rem(gi + e, G)
+            if relief:
+
+                @pl.when(end)
+                def _():
+                    close_product(2 + ci, r)
+
+            if ci == 0:
+
+                @pl.when(e == 1)
+                def _():
+                    for j in range(1, G):
+                        yu_copy(j, True).wait_recv()
+
+            @pl.loop(0, blocks // together)
+            def _(i):
+                running = [attend(r, i * together + j, ci) for j in range(together)]
+                for step in zip(*running):
+                    for store in [store for stores in step for store in stores or ()]:
+                        store()
 
     def part_copy(j, arriving):
         peer = lax.rem(t + nt - j, nt) if arriving else lax.rem(t + j, nt)
@@ -588,15 +661,15 @@
 
     def up_copy(ci, e, a):
         there = lax.rem(gi + e, G)
-        src = upv_send.at[there, a] if ci == 2 else upq_send.at[ci, there, a]
-        dst = upv_got.at[me, gi] if ci == 2 else upq_got.at[ci, me, gi]
+        src = upv_send.at[there, a] if ci > last else upq_send[ci].at[there, a]
+        dst = upv_got.at[me, gi] if ci > last else upq_got[ci].at[me, gi]
         return remote(
             src, dst, us_send.at[ci, e, a], us_recv.at[ci, me, gi], at_group(there, dp=a)
         )
 
     def up_arrival(ci, e, s):
         there = lax.rem(gi + e, G)
-        dst = upv_got.at[s, there] if ci == 2 else upq_got.at[ci, s, there]
+        dst = upv_got.at[s, there] if ci > last else upq_got[ci].at[s, there]
         return remote(dst, dst, us_send.at[ci, e, s], us_recv.at[ci, s, there], at_group(there, dp=s))
 
     def others(body):
@@ -613,12 +686,12 @@
                     body(e, a)
 
     def send_ups(ci):
-        if ci == 2:
+        if ci > last:
             upv_send[...] = upv_sum[...].astype(jnp.bfloat16)
             upv_got[me, gi] = upv_send[gi, me]
         else:
-            upq_send[ci] = upq_sum[ci].astype(jnp.bfloat16)
-            upq_got[ci, me, gi] = upq_send[ci, gi, me]
+            upq_send[ci][...] = upq_sum[ci][...].astype(jnp.bfloat16)
+            upq_got[ci][me, gi] = upq_send[ci][gi, me]
         others(lambda e, a: up_copy(ci, e, a).start())
 
     with jax.named_scope("start"):
@@ -635,7 +708,7 @@
             def _():
                 end_meta().start()
 
-        loads[8].wait()
+        loads[6].wait()
         for j in range(1, G):
             for k in range(TOKEN_SUBS):
                 yt_copy(j, k, False).start()
@@ -647,7 +720,7 @@
             for copy in y_copies(j, True)[:3]:
                 copy.wait_recv()
         send_own(FACTORS, (1,))
-        for copy in loads[6:8]:
+        for copy in loads[8:]:
             copy.wait()
         if relief:
 
@@ -661,21 +734,29 @@
             @pl.when(end)
             def _():
                 send_own(2)
+                send_own(3)
                 end_down().start()
-                send_own(3)
-
-        upq_sum[...] = jnp.zeros_like(upq_sum)
+                send_own(4)
+
+        for ref in upq_sum:
+            ref[...] = jnp.zeros_like(ref)
         upv_sum[...] = jnp.zeros_like(upv_sum)
-        loads[9].wait()
+        loads[7].wait()
     other_planes = [lax.rem(gi + j, G) for j in range(1, G)]
-    with jax.named_scope("line0"):
-        keys_of = [(1, None), (2, 1)]
-        line(0, hooks=[(keys_of[k], functools.partial(relay_tokens, k)) for k in range(TOKEN_SUBS)])
-
+    inward_only = False if relief else None
+
+    def next_own(item, to_end):
         @pl.when(~end)
         def _():
-            send_own(2)
-
+            send_own(item, to_end=to_end)
+
+    def after_first():
+        next_own(2, None)
+        relay_tokens(0)
+
+    with jax.named_scope("line0"):
+        relays = [((2, 1), functools.partial(relay_tokens, k)) for k in range(1, TOKEN_SUBS)]
+        line(0, hooks=[((1, None), after_first)] + relays)
     if relief:
         with jax.named_scope("relay_extra"):
 
@@ -689,20 +770,25 @@
                         ey_copy(j, k, False).start()
                     spread_tokens(gi, k, 1)
 
-    with jax.named_scope("pass"):
+    def pass_other():
         for r in other_planes:
             pass_tokens(r)
+
     with jax.named_scope("linef"):
-        line(FACTORS, hooks=[((n - 1, None), down_parts)])
+        line(FACTORS, hooks=[((1, None), pass_other), ((n - 1, 1), down_parts)])
         if relief:
 
             @pl.when(near)
             def _():
-                send_own(3, to_end=True)
-
+                for item in range(3, 3 + last):
+                    send_own(item, to_end=True)
 
     def extra_pass():
+        if last:
+            next_own(3, inward_only)
         if relief:
+            forward_ends(3)
+            next_own(4, inward_only)
 
             @pl.when(near)
             def _():
@@ -726,10 +812,6 @@
     with jax.named_scope("line2"):
         line(2, hooks=[((1, None), extra_pass), ((2, None), tokens_done)])
 
-        @pl.when(~end)
-        def _():
-            send_own(3, to_end=False if relief else None)
-
     if relief:
         with jax.named_scope("far_sums"):
 
@@ -738,120 +820,84 @@
                 settle_tokens(gi, 1)
                 far_sums(2, gi)
 
-    with jax.named_scope("whole2"):
-
+    @pl.when(~end)
+    def _():
+        for ci in range(1, last + 1):
+            slice_product(2 + ci, me, True)
+
+    def before_attention():
         @pl.when(~end)
         def _():
             for e in range(G):
                 whole_product(2, lax.rem(gi + e, G))
-            for j in range(1, G):
-                yu_copy(j, True).wait_recv()
-
-            slice_product(3, me, True)
 
         for j in range(1, G):
             y_copies(j, True)[3].wait_recv()
-    total_blocks = G * blocks
-    steps = (n - 1) * SUBS
-    per = -(-total_blocks // SUBS)
-    per_end = -(-total_blocks // (2 * SUBS))
-
-    def first_unit(k):
-        index = lax.rem(gi + lax.div(k, blocks), G) * blocks + lax.rem(k, blocks)
-        prepare(index)
-        attend(index, 0)
-
-    def near_step(i):
-        @pl.when(i == 0)
-        def _():
-            remote(x_down, x_down, eu_send, eu_recv, {"dp": outward}).wait_recv()
-            down_product(G, x_down, parts_extra)
-            for j in range(1, nt):
-                px_copy(j, False).start()
-            for r in other_planes:
-                pass_tokens(r, 1)
-
-        @pl.when(i == 1)
-        def _():
-            for j in range(1, nt):
-                px_copy(j, True).wait_recv()
-            down_sum(G, parts_extra)
-            ue_copy().start()
-
-        @pl.when(i == 2)
-        def _():
-            for r in other_planes:
-                settle_tokens(r, 1)
-                far_sums(2, r)
-
-    def end_step(i):
-        @pl.when(i == SUBS)
-        def _():
-            finish_down()
-            close_product(2, gi)
-
-        @pl.when(i == 2 * SUBS)
-        def _():
-            for r in other_planes:
-                close_product(2, r)
-            for j in range(1, G):
-                yu_copy(j, True).wait_recv()
-
-    with jax.named_scope("line3"):
-
-        @pl.loop(0, steps)
-        def _(i):
-            d, p = lax.div(i, SUBS) + 1, lax.rem(i, SUBS)
-            forward_piece(3, d, p, 0)
-
-            @pl.when(p == SUBS - 1)
-            def _():
-                for way in (0, 1):
-                    s = me - d if way == 0 else me + d
-
-                    @pl.when(((s >= 0) if way == 0 else (s < n)) & ~end)
-                    def _():
-                        slice_product(3, s, False)
-
-            if relief:
-                pl.when(near)(lambda: near_step(i))
-                pl.when(end)(lambda: end_step(i))
-                start = jnp.where(end, (i - SUBS) * per_end, i * per)
-                count = jnp.where(end, per_end, per)
-            else:
-                start, count = i * per, per
-
-            @pl.loop(0, max(per, per_end))
-            def _(j):
-                @pl.when((j < count) & (start + j >= 0) & (start + j < total_blocks))
+        if relief:
+
+            @pl.when(near)
+            def _():
+                for r in other_planes:
+                    pass_tokens(r, 1)
+                    settle_tokens(r, 1)
+                    far_sums(2, r)
+
+            @pl.when(end)
+            def _():
+                finish_down()
+
+    def extra_down():
+        remote(x_down, x_down, eu_send, eu_recv, {"dp": outward}).wait_recv()
+        down_product(G, x_down, parts_extra)
+        for j in range(1, nt):
+            px_copy(j, False).start()
+
+    def extra_down_sum():
+        for j in range(1, nt):
+            px_copy(j, True).wait_recv()
+        down_sum(G, parts_extra)
+        ue_copy().start()
+
+    if not last:
+        before_attention()
+    for ci in range(1, last + 1):
+        item = 2 + ci
+
+        def products(d):
+            for way in (0, 1):
+                s = me - d if way == 0 else me + d
+
+                @pl.when(((s >= 0) if way == 0 else (s < n)) & ~end)
                 def _():
-                    first_unit(start + j)
-
-        if not steps:
-            pl.loop(0, total_blocks)(first_unit)
+                    slice_product(item, s, False)
+
+        def between_distances():
+            if ci < last and not relief:
+                next_own(item + 1, inward_only)
+            if ci == 1:
+                before_attention()
+            if relief and ci == 1:
+                pl.when(near)(extra_down)
+            with jax.named_scope("att"):
+                attend_chunk(ci - 1)
+            if relief and ci == 1:
+                forward_ends(4)
+                pl.when(near)(extra_down_sum)
+
+        with jax.named_scope(f"line{item}"):
+            line(item, after=products, hooks=[((1, None), between_distances)])
+        if relief:
+
+            @pl.when(near)
+            def _():
+                for e in range(G):
+                    far_sums(item, lax.rem(gi + e, G))
+
+    with jax.named_scope("ups"):
+        for ci in range(last):
+            send_ups(ci)
     with jax.named_scope("tail_attend"):
-        if relief:
-
-            @pl.when(near)
-            def _():
-                for e in range(G):
-                    far_sums(3, lax.rem(gi + e, G))
-
-        send_ups(0)
-
-        @pl.loop(0, G)
-        def _(e):
-            r = lax.rem(gi + e, G)
-            if relief:
-
-                @pl.when(end)
-                def _():
-                    close_product(3, r)
-
-            @pl.loop(0, blocks)
-            def _(b):
-                attend(r * blocks + b, 1)
-                finish_values(r * blocks + b)
+        attend_chunk(last)
 
     with jax.named_scope("back"):
         for r in range(G):
@@ -877,8 +923,8 @@
     with jax.named_scope("backx"):
         for e, j in crossing:
             back_copy(e, j, False).start()
-        send_ups(1)
-        send_ups(2)
+        send_ups(last)
+        send_ups(last + 1)
         back_got[gi, t] = back_send[gi]
         for e, j in crossing:
             back_copy(e, j, True).wait_recv()
@@ -929,16 +975,19 @@
         low_got[me] = low_send[me]
 
     with jax.named_scope("upsum"):
-        for ci in range(3):
+        for ci in range(last + 2):
             others(lambda e, s: up_arrival(ci, e, s).wait_recv())
+        at = 2 * width
         for e in range(G):
-            for ci in range(2):
-                out = jnp.zeros((R, hc), jnp.float32)
-                out = lax.fori_loop(0, n, lambda s, v: v + upq_got[ci, s, e].astype(jnp.float32), out)
-                upq_out[:, e * hq + ci * hc : e * hq + (ci + 1) * hc] = out
+            for ci in range(last + 1):
+                out = jnp.zeros((R, widths[ci]), jnp.float32)
+                out = lax.fori_loop(
+                    0, n, lambda s, v: v + upq_got[ci][s, e].astype(jnp.float32), out
+                )
+                out_ref[:, at + e * hq + starts[ci] : at + e * hq + starts[ci] + widths[ci]] = out
             out = jnp.zeros((R, hk), jnp.float32)
             out = lax.fori_loop(0, n, lambda s, v: v + upv_got[s, e].astype(jnp.float32), out)
-            upv_out[:, e * hk : (e + 1) * hk] = out
+            out_ref[:, at + qcols + e * hk : at + qcols + (e + 1) * hk] = out
 
     with jax.named_scope("lowx"):
         @pl.loop(0, n)
@@ -949,15 +998,14 @@
                     low_got.at[s], low_got.at[s], lo_send.at[s], lo_recv.at[s], {"dp": s}
                 ).wait_recv()
 
-        for i, out in enumerate((lowq_out, lowv_out)):
-            out[...] = jnp.zeros_like(out)
-
-            @pl.loop(0, n)
-            def _(s):
-                out[...] += low_got[s, i * R : (i + 1) * R, :].astype(jnp.float32)
-
-    with jax.named_scope("drain"):
-        for item in range(4):
+        for i in range(2):
+            out = jnp.zeros((R, width), jnp.float32)
+            out = lax.fori_loop(
+                0, n, lambda s, v: v + low_got[s, i * R : (i + 1) * R, :].astype(jnp.float32), out
+            )
+            out_ref[:, i * width : (i + 1) * width] = out
+
+        for item in range(3 + last):
 
             @pl.loop(0, n)
             def _(s):
@@ -997,8 +1045,8 @@
                         ey_copy(j, k, False).wait_send()
                 for e in range(G):
                     drain_tokens(e, 1)
-                    pp_copy(2, e).wait_send()
-                    pp_copy(3, e).wait_send()
+                    for item in range(2, 3 + last):
+                        pp_copy(item, e).wait_send()
                 for j in range(1, nt):
                     px_copy(j, False).wait_send()
                 ue_copy().wait_send()
@@ -1010,7 +1058,7 @@
 
         for e, j in crossing:
             back_copy(e, j, False).wait_send()
-        for ci in range(3):
+        for ci in range(last + 2):
             others(lambda e, a: up_copy(ci, e, a).wait_send())
 
         @pl.loop(0, n)
@@ -1027,7 +1075,7 @@
     kcols = wk.shape[1]
     width = aq.shape[1]
     hq, hk = qcols // G, kcols // G
-    hc = hq // 2
+    widths = [c * HD for c in query_chunks(hq // HD)]
     span = n * depth
     blocks = rows // REQUEST_ROWS
     far = (n - 2) * depth
@@ -1047,35 +1095,30 @@
     return pl.pallas_call(
         functools.partial(layer_kernel, G, relief),
         out_shape=(
-            jax.ShapeDtypeStruct((R, width), f32),
-            jax.ShapeDtypeStruct((R, width), f32),
-            jax.ShapeDtypeStruct((R, qcols), f32),
-            jax.ShapeDtypeStruct((R, kcols), f32),
+            jax.ShapeDtypeStruct((R, 2 * width + qcols + kcols), f32)
         ),
         in_specs=[smem] * 4 + [hbm] * 9 + [vmem] * 2,
-        out_specs=(vmem,) * 4,
+        out_specs=vmem,
         scratch_shapes=[
             V((G, rows, span), bf),
             V((span, 2 * hk), bf),
-            V((span, hc), bf),
-            V((span, hc), bf),
+            [V((span, w), bf) for w in widths],
             V((n, 2 * R, width), bf),
             V((n, G, R, hq + hk), bf),
             V((G, rows, hq), bf),
             V((G, rows, 2 * hk), f32),
-            V((G, rows, hc), f32),
-            V((G, rows, hc), f32),
+            [V((G, rows, w), f32) for w in widths],
             V((nt, 2 * R, rows), f32),
             V((G + 1, 2 * R, rows), bf),
             V((G, rows, hk), bf),
             V((G, rows, hk), bf),
             V((G, rows, hk), f32),
             V((G, 2 * R, rows), f32),
-            V((2, G, n, R, hc), f32),
+            [V((G, n, R, w), f32) for w in widths],
             V((G, n, R, hk), f32),
-            V((2, G, n, R, hc), bf),
+            [V((G, n, R, w), bf) for w in widths],
             V((G, n, R, hk), bf),
-            V((2, n, G, R, hc), bf),
+            [V((n, G, R, w), bf) for w in widths],
             V((n, G, R, hk), bf),
             V((G, 2 * R, rows), bf),
             V((G, nt, 2 * R, rows), bf),
@@ -1085,20 +1128,18 @@
             V((G, rows, far) if relief else (1, 16, 128), bf),
             V((rows, width) if relief else (16, 128), bf),
             V((nt, 2 * R, rows) if relief else (1, 8, 128), f32),
-            V((G, rows, hc) if relief else (1, 16, 128), bf),
-            V((G, rows, hc) if relief else (1, 16, 128), bf),
-            V((G, rows, hc) if relief else (1, 16, 128), bf),
-            V((G, rows, hc) if relief else (1, 16, 128), bf),
+            [V((G, rows, w) if relief else (1, 16, 128), bf) for w in widths],
+            [V((G, rows, w) if relief else (1, 16, 128), bf) for w in widths],
         ]
-        + pairs_of((10,))[:1]
-        + [dma((2, 4, n, SUBS)), dma((4, n, SUBS))]
+        + [dma((8 + len(widths),))]
+        + [dma((2, 2 + len(widths), n, SUBS)), dma((2 + len(widths), n, SUBS))]
         + pairs_of((G, 4))
         + pairs_of((G, TOKEN_SUBS))
         + pairs_of((2 * G, max(1, nt // 2), TOKEN_SUBS))
         + pairs_of((2 * G, nt, TOKEN_SUBS))
         + pairs_of((nt,))
         + pairs_of((G,))
-        + [dma((3, G, n)), dma((3, n, G))]
+        + [dma((1 + len(widths), G, n)), dma((1 + len(widths), n, G))]
         + pairs_of((G, nt))
         + pairs_of((n,))
         + [dma, dma]
@@ -1107,7 +1148,7 @@
         + [dma, dma]
         + pairs_of((nt,))
         + [dma, dma]
-        + pairs_of((2, G)),
+        + pairs_of((len(widths), G)),
         compiler_params=pltpu.CompilerParams(
             collective_id=0, has_side_effects=True, vmem_limit_bytes=62 * 1024 * 1024
         ),
@@ -1133,11 +1174,15 @@
     ng, nt = lax.axis_size("groups"), lax.axis_size("tensor")
     kv_heads = w_key.shape[1] // HD
     G = ng if nt % 2 == 0 and kv_heads % ng == 0 else 1
-    relief = G > 1 and lax.axis_size("dp") >= 4
-    low_q, low_v, up_q, up_v = layer(
+    chunks = len(query_chunks(w_query.shape[1] // G // HD))
+    relief = G > 1 and lax.axis_size("dp") >= 4 and chunks == 3
+    out = layer(
         G, relief, tokens, w_query, w_key, w_value, a_query[0].T, a_value[0].T, b_query[0], b_value[0],
         d_heads, block_adapter.reshape(-1), adapter_slot, adapter_ranks, live_tokens,
     )
+    width, qcols = a_query.shape[1], b_query.shape[2]
+    low_q, low_v = out[:, :width], out[:, width : 2 * width]
+    up_q, up_v = out[:, 2 * width : 2 * width + qcols], out[:, 2 * width + qcols :]
     return low_q.T[None], up_q[None], low_v.T[None], up_v[None]
 
 

time: 142 us -> 134 us (0.944)
  Pallas kernels: 133 us -> 129 us
  local copies, waits for them, and re-layouts: 6.08 us -> 3.16 us
    unnamed x4 -> x0, local copies, waits for them, and re-layouts: 6.08 us -> none
    pallas_call x1, Pallas kernels: 133 us -> 129 us  [layer(): pl.pallas_call(functools.partial(layer_kernel, G, relief), out_shape=jax....]
    broadcast_in_dim x0 -> x2, local copies, waits for them, and re-layouts: none -> 3.16 us  [on_device(): return (low_q.T[None], up_q[None], low_v.T[None], up_v[None])]
where the time goes in v3:
time: 134 us
  Pallas kernels  129 us (96%)
  local copies, waits for them, and re-layouts  3.16 us (2%)
    pallas_call x1, Pallas kernels, layer(): pl.pallas_call(functools.partial(layer_kernel, G, relief), out_shape=jax....  129 us
    broadcast_in_dim x2, local copies, waits for them, and re-layouts, on_device(): return (low_q.T[None], up_q[None], low_v.T[None], up_v[None])  3.16 us

profile of v3, /device:TPU:24, one launch (start us, length us, event | category | flops | bytes accessed | tf_op | source)
XLA Modules:
  0.0 133.5 jit_solution(11691114857514396840)
XLA Ops:
  1.3 129.1 %layer.1 = f32[32,3328]{1,0:T(8,128)} custom-call(s32[4]{0:T(128)} %bitcast.25, s32[4]{0:T(128)} %slot_ref.1, s32[4]{0:T(128)} %rank_ref.1, s32[1]{0:T(128)S(6)} %copy.19.live_ref, bf16[512,4096]{1,0:T(8,128)(2,1)} %x_hbm.1, bf16[1024,1024]{1,0:T(8,128)(2,1)} %wq_hbm.1, bf16[1024,256]{1,0:T(8,128)(2,1)} %wk_hbm.1, bf16[1024,256]{1,0:T(8,128)(2,1)} %wv_hbm.1, ...), custom_call_target="tpu_custom_call" | custom-call | tf_op jit(solution)/shard_map/layer/pallas_call | solution.py:1095
  130.3 1.8 %slice_bitcast_fusion = (f32[1,1024,32]{1,2,0:T(8,128)}, f32[1,32,1024]{2,1,0:T(8,128)}, f32[1,1024,32]{1,2,0:T(8,128)}) fusion(f32[32,3328]{1,0:T(8,128)} %layer.1), kind=kLoop, calls=%fused_computation | loop fusion | bytes 786432 | tf_op jit(solution)/shard_map/broadcast_in_dim | solution.py:1186
  132.1 1.4 %slice_bitcast_fusion.3 = f32[1,32,256]{2,1,0:T(8,128)} fusion(f32[32,3328]{1,0:T(8,128)} %layer.1), kind=kLoop, calls=%fused_computation.3 | loop fusion | bytes 65536 | tf_op jit(solution)/shard_map/broadcast_in_dim | solution.py:1186

commit v4 on v3

--- a/solution.py
+++ b/solution.py
@@ -84,6 +84,7 @@
     upv_got,
     back_send,
     back_got,
+    back_all,
     low_send,
     low_got,
     meta,
@@ -127,6 +128,8 @@
     ue_recv,
     pp_send,
     pp_recv,
+    ba_send,
+    ba_recv,
 ):
     n = lax.axis_size("dp")
     ng = lax.axis_size("groups")
@@ -435,17 +438,32 @@
 
     def close_product(item, r):
         close = pl.ds(pl.multiple_of(close_of_end, 128), 2 * depth)
-        remote(
-            p_got[item - 2].at[r], p_got[item - 2].at[r], pp_send.at[item - 2, r], pp_recv.at[item - 2, r],
-            {"dp": inward},
-        ).wait_recv()
 
         @pl.loop(0, rows // tile)
         def _(i):
             span = pl.ds(pl.multiple_of(i * tile, tile), tile)
             accs[item][r, span, :] = jnp.dot(
                 x_all[r, span, close], weights[item][close, :], preferred_element_type=jnp.float32
-            ) + p_got[item - 2][r, span, :].astype(jnp.float32)
+            )
+
+    def close_products(item):
+        if relief:
+
+            @pl.when(end)
+            def _():
+                for r in range(G):
+                    close_product(item, r)
+
+    def add_far_sums(item, r):
+        remote(
+            p_got[item - 2].at[r], p_got[item - 2].at[r], pp_send.at[item - 2, r], pp_recv.at[item - 2, r],
+            {"dp": inward},
+        ).wait_recv()
+
+        @pl.loop(0, rows // tile)
+        def _(i):
+            span = pl.ds(pl.multiple_of(i * tile, tile), tile)
+            accs[item][r, span, :] += p_got[item - 2][r, span, :].astype(jnp.float32)
 
     def slice_product(item, s, first):
         k_span = pl.ds(pl.multiple_of(s * depth, 128), depth)
@@ -593,7 +611,7 @@
 
                 @pl.when(end)
                 def _():
-                    close_product(2 + ci, r)
+                    add_far_sums(2 + ci, r)
 
             if ci == 0:
 
@@ -858,12 +876,20 @@
         down_sum(G, parts_extra)
         ue_copy().start()
 
+    close_products(2)
     if not last:
         before_attention()
     for ci in range(1, last + 1):
         item = 2 + ci
 
         def products(d):
+            if relief and d == n - 2:
+
+                @pl.when(near)
+                def _():
+                    for e in range(G):
+                        far_sums(item, lax.rem(gi + e, G))
+
             for way in (0, 1):
                 s = me - d if way == 0 else me + d
 
@@ -872,6 +898,7 @@
                     slice_product(item, s, False)
 
         def between_distances():
+            close_products(item)
             if ci < last and not relief:
                 next_own(item + 1, inward_only)
             if ci == 1:
@@ -886,12 +913,6 @@
 
         with jax.named_scope(f"line{item}"):
             line(item, after=products, hooks=[((1, None), between_distances)])
-        if relief:
-
-            @pl.when(near)
-            def _():
-                for e in range(G):
-                    far_sums(item, lax.rem(gi + e, G))
 
     with jax.named_scope("ups"):
         for ci in range(last):
@@ -901,7 +922,8 @@
 
     with jax.named_scope("back"):
         for r in range(G):
-            back_send[r] = back_acc[r].astype(jnp.bfloat16)
+            for q in range(nt):
+                back_send[r, q] = back_acc[r, :, q * quarter : (q + 1) * quarter].astype(jnp.bfloat16)
 
     def back_copy(e, j, arriving):
         there = lax.rem(gi + e, G)
@@ -912,26 +934,37 @@
                 dst, dst, bk_send.at[e, j], bk_recv.at[there, peer], at_group(there, tensor=peer)
             )
         return remote(
-            back_send.at[there],
+            back_send.at[there, peer],
             back_got.at[gi, t],
             bk_send.at[e, j],
             bk_recv.at[gi, t],
             at_group(there, tensor=peer),
         )
 
+    def all_copy(j, arriving):
+        peer = lax.rem(t + nt - j, nt) if arriving else lax.rem(t + j, nt)
+        ref = back_all.at[peer if arriving else t]
+        return remote(ref, ref, ba_send.at[j], ba_recv.at[j], {"tensor": peer})
+
     crossing = [(e, j) for e in range(G) for j in range(nt) if (e, j) != (0, 0)]
     with jax.named_scope("backx"):
         for e, j in crossing:
             back_copy(e, j, False).start()
+        back_got[gi, t] = back_send[gi, t]
+        for e, j in crossing:
+            back_copy(e, j, True).wait_recv()
+        total = jnp.zeros(back_got.shape[2:], jnp.float32)
+        for r in range(G):
+            for j in range(nt):
+                total = total + back_got[r, j].astype(jnp.float32)
+        back_all[t] = total.astype(jnp.bfloat16)
+        for j in range(1, nt):
+            all_copy(j, False).start()
         send_ups(last)
         send_ups(last + 1)
-        back_got[gi, t] = back_send[gi]
-        for e, j in crossing:
-            back_copy(e, j, True).wait_recv()
-    total = jnp.zeros(back_acc.shape[1:], jnp.float32)
-    for r in range(G):
-        for j in range(nt):
-            total = total + back_got[r, j].astype(jnp.float32)
+        for j in range(1, nt):
+            all_copy(j, True).wait_recv()
+    total = jnp.concatenate([back_all[q] for q in range(nt)], axis=1).astype(jnp.float32)
     kept = []
     for b in range(blocks):
         span = slice(b * REQUEST_ROWS, (b + 1) * REQUEST_ROWS)
@@ -1058,6 +1091,8 @@
 
         for e, j in crossing:
             back_copy(e, j, False).wait_send()
+        for j in range(1, nt):
+            all_copy(j, False).wait_send()
         for ci in range(last + 2):
             others(lambda e, a: up_copy(ci, e, a).wait_send())
 
@@ -1120,8 +1155,9 @@
             V((G, n, R, hk), bf),
             [V((n, G, R, w), bf) for w in widths],
             V((n, G, R, hk), bf),
-            V((G, 2 * R, rows), bf),
-            V((G, nt, 2 * R, rows), bf),
+            V((G, nt, 2 * R, rows // nt), bf),
+            V((G, nt, 2 * R, rows // nt), bf),
+            V((nt, 2 * R, rows // nt), bf),
             V((n, 2 * R, width), bf),
             V((n, 2 * R, width), bf),
             pltpu.SMEM((G + 1, 128), jnp.int32),
@@ -1148,7 +1184,8 @@
         + [dma, dma]
         + pairs_of((nt,))
         + [dma, dma]
-        + pairs_of((len(widths), G)),
+        + pairs_of((len(widths), G))
+        + pairs_of((nt,)),
         compiler_params=pltpu.CompilerParams(
             collective_id=0, has_side_effects=True, vmem_limit_bytes=62 * 1024 * 1024
         ),

time: 134 us -> 131 us (0.978)
  Pallas kernels: 129 us -> 126 us
    pallas_call x1, Pallas kernels: 129 us -> 126 us  [layer(): pl.pallas_call(functools.partial(layer_kernel, G, relief), out_shape=jax....]
where the time goes in v4:
time: 131 us; the launch traced here: 130 us
  Pallas kernels  126 us (96%)
  local copies, waits for them, and re-layouts  3.16 us (2%)
    pallas_call x1, Pallas kernels, layer(): pl.pallas_call(functools.partial(layer_kernel, G, relief), out_shape=jax....  126 us
    broadcast_in_dim x2, local copies, waits for them, and re-layouts, on_device(): return (low_q.T[None], up_q[None], low_v.T[None], up_v[None])  3.16 us

profile of v4, /device:TPU:24, one launch (start us, length us, event | category | flops | bytes accessed | tf_op | source)
XLA Modules:
  0.0 130.3 jit_solution(17657136077090884343)
XLA Ops:
  1.3 125.9 %layer.1 = f32[32,3328]{1,0:T(8,128)} custom-call(s32[4]{0:T(128)} %bitcast.25, s32[4]{0:T(128)} %slot_ref.1, s32[4]{0:T(128)} %rank_ref.1, s32[1]{0:T(128)S(6)} %copy.19.live_ref, bf16[512,4096]{1,0:T(8,128)(2,1)} %x_hbm.1, bf16[1024,1024]{1,0:T(8,128)(2,1)} %wq_hbm.1, bf16[1024,256]{1,0:T(8,128)(2,1)} %wk_hbm.1, bf16[1024,256]{1,0:T(8,128)(2,1)} %wv_hbm.1, ...), custom_call_target="tpu_custom_call" | custom-call | tf_op jit(solution)/shard_map/layer/pallas_call | solution.py:1130
  127.2 1.8 %slice_bitcast_fusion = (f32[1,1024,32]{1,2,0:T(8,128)}, f32[1,32,1024]{2,1,0:T(8,128)}, f32[1,1024,32]{1,2,0:T(8,128)}) fusion(f32[32,3328]{1,0:T(8,128)} %layer.1), kind=kLoop, calls=%fused_computation | loop fusion | bytes 786432 | tf_op jit(solution)/shard_map/broadcast_in_dim | solution.py:1223
  129.0 1.4 %slice_bitcast_fusion.3 = f32[1,32,256]{2,1,0:T(8,128)} fusion(f32[32,3328]{1,0:T(8,128)} %layer.1), kind=kLoop, calls=%fused_computation.3 | loop fusion | bytes 65536 | tf_op jit(solution)/shard_map/broadcast_in_dim | solution.py:1223

commit v5 on v4

--- a/solution.py
+++ b/solution.py
@@ -16,7 +16,7 @@
 adapter_alpha_factor = 32.0
 rope_theta = 500000.0
 
-SUBS = 4
+SUBS = 2
 TOKEN_SUBS = 2
 FACTORS = 1
 

time: 131 us -> 129 us (0.985)
  Pallas kernels: 126 us -> 124 us
    pallas_call x1, Pallas kernels: 126 us -> 124 us  [layer(): pl.pallas_call(functools.partial(layer_kernel, G, relief), out_shape=jax....]
where the time goes in v5:
time: 129 us
  Pallas kernels  124 us (96%)
  local copies, waits for them, and re-layouts  3.16 us (2%)
  between operations  1.29 us (1%)
    pallas_call x1, Pallas kernels, layer(): pl.pallas_call(functools.partial(layer_kernel, G, relief), out_shape=jax....  124 us
    broadcast_in_dim x2, local copies, waits for them, and re-layouts, on_device(): return (low_q.T[None], up_q[None], low_v.T[None], up_v[None])  3.16 us

profile of v5, /device:TPU:24, one launch (start us, length us, event | category | flops | bytes accessed | tf_op | source)
XLA Modules:
  0.0 128.9 jit_solution(9383567702974527305)
XLA Ops:
  1.3 124.5 %layer.1 = f32[32,3328]{1,0:T(8,128)} custom-call(s32[4]{0:T(128)} %bitcast.25, s32[4]{0:T(128)} %slot_ref.1, s32[4]{0:T(128)} %rank_ref.1, s32[1]{0:T(128)S(6)} %copy.19.live_ref, bf16[512,4096]{1,0:T(8,128)(2,1)} %x_hbm.1, bf16[1024,1024]{1,0:T(8,128)(2,1)} %wq_hbm.1, bf16[1024,256]{1,0:T(8,128)(2,1)} %wk_hbm.1, bf16[1024,256]{1,0:T(8,128)(2,1)} %wv_hbm.1, ...), custom_call_target="tpu_custom_call" | custom-call | tf_op jit(solution)/shard_map/layer/pallas_call | solution.py:1130
  125.8 1.8 %slice_bitcast_fusion = (f32[1,1024,32]{1,2,0:T(8,128)}, f32[1,32,1024]{2,1,0:T(8,128)}, f32[1,1024,32]{1,2,0:T(8,128)}) fusion(f32[32,3328]{1,0:T(8,128)} %layer.1), kind=kLoop, calls=%fused_computation | loop fusion | bytes 786432 | tf_op jit(solution)/shard_map/broadcast_in_dim | solution.py:1223
  127.5 1.4 %slice_bitcast_fusion.3 = f32[1,32,256]{2,1,0:T(8,128)} fusion(f32[32,3328]{1,0:T(8,128)} %layer.1), kind=kLoop, calls=%fused_computation.3 | loop fusion | bytes 65536 | tf_op jit(solution)/shard_map/broadcast_in_dim | solution.py:1223
